TPU v7x, 32 devices: a whole 2x2x4 slice. The times are simulated.
32 devices in a mesh: seq: 8 (over z, y), head: 4 (over x, core).
Axes of the slice: x: 2, y: 2, z: 4, core: 2. Of those that a mesh axis runs over, the one named last changes fastest.
Arguments:
- patches: bfloat16 [2048, 1280], P('seq'), may hold values from -6 to 6
- norm_gain: float32 [1280], replicated, may hold values from 0.5 to 1.5
- w_qkv: bfloat16 [1280, 3, 1280], P('seq', None, 'head'), as said below
- w_out: bfloat16 [1280, 1280], P('head', 'seq'), may hold values from -0.15625 to 0.15625
- window_order: int32 [8, 64], P('seq'), may hold values from 0 to 63, each once within a row
- merge_gain: float32 [1280], replicated, may hold values from 0.5 to 1.5
- w_kv: bfloat16 [5120, 2, 1024], P('seq', None, 'head'), as said below
- queries: bfloat16 [16, 8192], P('seq', 'head'), may hold values from -6 to 6
- suffix_kv: bfloat16 [16, 64, 2, 1024], P('seq', None, None, 'head'), may hold values from -12 to 12
- question_lengths: int32 [16], P('seq'), may hold values from 1 to 64
- frame_range: int32 [16, 2], replicated, may hold values from 0 to 8, as said below
Outputs:
- answers: bfloat16 [16, 8192], P('seq', 'head')
Inputs may be any that keep to these rules, and one draw needn't show every extreme that they name: `window_order`: each row is an ordering of a frame's units; positions w * 16 to (w + 1) * 16 - 1 form window w. `frame_range`: the first entry of a row is below the second. `w_qkv`: entries of order one over the square root of 1280. `w_kv`: entries of order one over the square root of 5120.
All inputs are finite; a program needn't handle non-finite values.
Results may differ from a plain program's by a relative error of at most 0.007.
Values may be sent and summed in bfloat16 or wider, within the bound.
A program may use at most 64 MiB of HBM per device.

v0:
```python
import functools

import jax
import jax.numpy as jnp
from jax import lax
from jax.experimental import pallas as pl
from jax.experimental.pallas import tpu as pltpu
from jax.sharding import PartitionSpec as P

VD = 1280
VH = 16
HD = 128
FPATCH = 256
WIN = 64

MESH = pl.DeviceIdType.MESH
VMEM = pl.BlockSpec(memory_space=pltpu.VMEM)


def rms_scale(values, gain):
    return values * lax.rsqrt(jnp.mean(values * values, axis=-1, keepdims=True) + 1e-06) * gain


def exchange_kernel(axis, count, gather, x_ref, out_ref, send_sem, recv_sem, own_sem):
    me = lax.axis_index(axis)
    barrier = pltpu.get_barrier_semaphore()
    for step in range(1, count):
        pl.semaphore_signal(
            barrier, inc=1, device_id={axis: lax.rem(me + step, count)}, device_id_type=MESH
        )
    pl.semaphore_wait(barrier, count - 1)
    copies = []
    for step in range(1, count):
        peer = lax.rem(me + step, count)
        copy = pltpu.make_async_remote_copy(
            src_ref=x_ref if gather else x_ref.at[peer],
            dst_ref=out_ref.at[me],
            send_sem=send_sem.at[step],
            recv_sem=recv_sem.at[step],
            device_id={axis: peer},
            device_id_type=MESH,
        )
        copy.start()
        copies.append(copy)
    own = pltpu.make_async_copy(x_ref if gather else x_ref.at[me], out_ref.at[me], own_sem)
    own.start()
    own.wait()
    for copy in copies:
        copy.wait()


def exchange(x, axis, gather, collective_id):
    count = lax.axis_size(axis)
    shape = ((count,) + x.shape) if gather else x.shape
    return pl.pallas_call(
        functools.partial(exchange_kernel, axis, count, gather),
        out_shape=jax.ShapeDtypeStruct(shape, x.dtype),
        in_specs=[VMEM],
        out_specs=VMEM,
        scratch_shapes=[
            pltpu.SemaphoreType.DMA((count,)),
            pltpu.SemaphoreType.DMA((count,)),
            pltpu.SemaphoreType.DMA,
        ],
        compiler_params=pltpu.CompilerParams(collective_id=collective_id, has_side_effects=True),
        name=f"exchange_{collective_id}",
    )(x)


def ring_kernel(count, qkv_ref, wout_ref, qkv_out, wout_out, send_sem, recv_sem, own_sem):
    me = lax.axis_index("seq")
    odd = lax.rem(me, 2)
    place = (1 - odd) * (me // 2) + odd * (count - 1 - me // 2)

    def index_of(position):
        position = lax.rem(position + count, count)
        late = position // (count // 2)
        return (1 - late) * 2 * position + late * (2 * (count - 1 - position) + 1)

    neighbours = (index_of(place + 1), index_of(place - 1))
    barrier = pltpu.get_barrier_semaphore()
    for neighbour in neighbours:
        pl.semaphore_signal(barrier, inc=1, device_id={"seq": neighbour}, device_id_type=MESH)
    pl.semaphore_wait(barrier, 2)
    far, near = count // 2, count - 1 - count // 2
    pieces = 4

    def slot(piece, source):
        return qkv_out.at[piece, source] if piece < 3 else wout_out.at[source]

    def own(piece):
        return qkv_ref.at[piece] if piece < 3 else wout_ref

    copies = {}
    for step in range(far):
        for piece in range(pieces):
            for way in range(2):
                hops = far if (piece < 2) == (way == 0) else near
                if step >= hops:
                    continue
                source = index_of(place - step if way == 0 else place + step)
                if step > 0:
                    copies[step - 1, piece, way].wait_recv()
                copy = pltpu.make_async_remote_copy(
                    src_ref=own(piece) if step == 0 else slot(piece, source),
                    dst_ref=slot(piece, source),
                    send_sem=send_sem.at[step, piece, way],
                    recv_sem=recv_sem.at[step, piece, way],
                    device_id={"seq": neighbours[way]},
                    device_id_type=MESH,
                )
                copy.start()
                copies[step, piece, way] = copy
    kept = [pltpu.make_async_copy(own(p), slot(p, me), own_sem.at[p]) for p in range(pieces)]
    for copy in kept:
        copy.start()
    for copy in kept:
        copy.wait()
    for (step, piece, way), copy in copies.items():
        if (step + 1, piece, way) not in copies:
            copy.wait_recv()
    for copy in copies.values():
        copy.wait_send()


def ring_weights(w_qkv, w_out):
    count = lax.axis_size("seq")
    far = count // 2
    return pl.pallas_call(
        functools.partial(ring_kernel, count),
        out_shape=(
            jax.ShapeDtypeStruct((3, count) + w_qkv.shape[1:], w_qkv.dtype),
            jax.ShapeDtypeStruct((count,) + w_out.shape, w_out.dtype),
        ),
        in_specs=[VMEM, VMEM],
        out_specs=(VMEM, VMEM),
        scratch_shapes=[
            pltpu.SemaphoreType.DMA((far, 4, 2)),
            pltpu.SemaphoreType.DMA((far, 4, 2)),
            pltpu.SemaphoreType.DMA((4,)),
        ],
        compiler_params=pltpu.CompilerParams(collective_id=0, has_side_effects=True),
        name="ring_weights",
    )(w_qkv, w_out)


def frame_attention(query, key, value, unit_order, head_size):
    unit_count = unit_order.shape[0]
    patch_count = unit_count * 4
    ranks = jnp.sum(
        jnp.where(
            unit_order[None, :] == (jnp.arange(patch_count) // 4)[:, None],
            jnp.arange(unit_count)[None, :] // (WIN // 4),
            0,
        ),
        axis=1,
    )
    same = ranks[:, None] == ranks[None, :]
    scores = jnp.einsum(
        "qhd,khd->hqk", query, key, preferred_element_type=jnp.float32
    ) * head_size ** (-0.5)
    scores = jnp.where(same[None], scores, -jnp.inf)
    weights = jax.nn.softmax(scores, axis=-1).astype(jnp.bfloat16)
    return jnp.einsum(
        "hqk,khd->qhd", weights, value, preferred_element_type=jnp.float32
    ).astype(jnp.bfloat16)


def on_device(
    patches,
    norm_gain,
    w_qkv,
    w_out,
    window_order,
    merge_gain,
    w_kv,
    queries,
    suffix_kv,
    question_lengths,
    frame_range,
):
    head_count = lax.axis_size("head")
    seq_count = lax.axis_size("seq")
    row_count = patches.shape[0]
    frame_count = window_order.shape[0]
    columns = w_qkv.shape[2]
    head_size = VD // VH
    local_heads = columns // head_size
    source = patches.astype(jnp.float32)
    normed = rms_scale(source, norm_gain).astype(jnp.bfloat16)
    qkv_all, w_out_all = ring_weights(w_qkv.transpose(1, 0, 2), w_out)
    qkv_all = qkv_all.reshape(3, -1, columns)
    query, key, value = [
        jnp.dot(normed, qkv_all[part], preferred_element_type=jnp.float32)
        .astype(jnp.bfloat16)
        .reshape(frame_count, -1, local_heads, head_size)
        for part in range(3)
    ]
    attended = jax.vmap(
        lambda q, k, v, order: frame_attention(q, k, v, order, head_size)
    )(query, key, value, window_order).reshape(row_count, columns)
    w_full = w_out_all.transpose(1, 0, 2).reshape(columns, VD)
    share_rows = row_count // head_count
    partial = jnp.dot(attended, w_full, preferred_element_type=jnp.float32).astype(jnp.bfloat16)
    parts = exchange(partial.reshape(head_count, share_rows, VD), "head", False, 1)
    shared = jnp.sum(parts.astype(jnp.float32), axis=0)
    own_rows = lax.dynamic_slice_in_dim(source, lax.axis_index("head") * share_rows, share_rows, 0)
    merged = rms_scale(own_rows + shared, merge_gain).astype(jnp.bfloat16)
    share_tokens = share_rows // 4
    depth = w_kv.shape[0]
    merged = merged.reshape(share_tokens, seq_count, depth).transpose(1, 0, 2)
    merged = exchange(merged, "seq", False, 2)
    merged = exchange(merged, "head", True, 3)
    merged = merged.transpose(1, 0, 2, 3).reshape(-1, depth)
    kv_columns = w_kv.shape[2]
    partial = jnp.dot(
        merged, w_kv.reshape(depth, 2 * kv_columns), preferred_element_type=jnp.float32
    ).astype(jnp.bfloat16)
    parts = exchange(partial.reshape(seq_count, -1, 2 * kv_columns), "seq", False, 4)
    visual = jnp.sum(parts.astype(jnp.float32), axis=0).astype(jnp.bfloat16)
    visual = exchange(visual, "seq", True, 5).reshape(-1, 2 * kv_columns)

    token_count = visual.shape[0]
    quest_count = queries.shape[0]
    span = suffix_kv.shape[1]
    kv_local = kv_columns // HD
    asking = queries.reshape(quest_count, kv_local, -1, HD)
    frame_tokens = FPATCH // 4
    seq_index = lax.axis_index("seq")
    bounds = lax.dynamic_slice_in_dim(frame_range, seq_index * quest_count, quest_count, 0)
    frame_index = jnp.arange(token_count) // frame_tokens
    live = (frame_index[None, :] >= bounds[:, 0:1]) & (frame_index[None, :] < bounds[:, 1:2])
    suffix_live = jnp.arange(span)[None, :] < question_lengths[:, None]
    suffix = suffix_kv.reshape(quest_count, span, 2, kv_local, HD)
    answers = []
    for g in range(kv_local):
        ask = asking[:, g]
        keys = visual[:, g * HD : (g + 1) * HD]
        values = visual[:, kv_columns + g * HD : kv_columns + (g + 1) * HD]
        scores = jnp.einsum(
            "qjd,nd->qjn", ask, keys, preferred_element_type=jnp.float32
        ) * HD ** (-0.5)
        scores = jnp.where(live[:, None, :], scores, -jnp.inf)
        tail = jnp.einsum(
            "qjd,qsd->qjs", ask, suffix[:, :, 0, g], preferred_element_type=jnp.float32
        ) * HD ** (-0.5)
        tail = jnp.where(suffix_live[:, None, :], tail, -jnp.inf)
        highest = jnp.maximum(
            jnp.max(scores, axis=-1, keepdims=True), jnp.max(tail, axis=-1, keepdims=True)
        )
        weights = jnp.exp(scores - highest)
        tail_weights = jnp.exp(tail - highest)
        totals = jnp.sum(weights, axis=-1, keepdims=True) + jnp.sum(
            tail_weights, axis=-1, keepdims=True
        )
        mixed = jnp.einsum(
            "qjn,nd->qjd", weights.astype(jnp.bfloat16), values, preferred_element_type=jnp.float32
        ) + jnp.einsum(
            "qjs,qsd->qjd",
            tail_weights.astype(jnp.bfloat16),
            suffix[:, :, 1, g],
            preferred_element_type=jnp.float32,
        )
        answers.append((mixed / totals).astype(jnp.bfloat16))
    return jnp.stack(answers, axis=1).reshape(quest_count, -1)


def solution(mesh):
    placed = (
        P("seq", None),
        P(),
        P("seq", None, "head"),
        P("head", "seq"),
        P("seq", None),
        P(),
        P("seq", None, "head"),
        P("seq", "head"),
        P("seq", None, None, "head"),
        P("seq"),
        P(),
    )
    return jax.shard_map(
        on_device, mesh=mesh, in_specs=placed, out_specs=P("seq", "head"), check_vma=False
    )
```

profile of v0, /device:TPU:0, one launch (start us, length us, event | category | flops | bytes accessed | tf_op | source)
XLA Modules:
  0.0 135.8 jit_solution(7043337956872746087)
XLA Ops:
  0.0 0.0 copy-start
  0.0 1.7 %copy.27.wout_ref = bf16[320,160]{1,0:T(8,128)(2,1)} copy(bf16[320,160]{0,1:T(8,128)(2,1)} %param.14) | data formatting | bytes 204800 | tf_op args[3]
  1.7 49.0 %ring_weights.1 = (bf16[3,8,160,320]{3,2,1,0:T(8,128)(2,1)}, bf16[8,320,160]{2,1,0:T(8,128)(2,1)}) custom-call(bf16[3,160,320]{2,1,0:T(8,128)(2,1)} %bitcast.133, bf16[320,160]{1,0:T(8,128)(2,1)} %copy.27.wout_ref), custom_call_target="tpu_custom_call" | custom-call | tf_op jit(solution)/shard_map/ring_weights/pallas_call | solution.py:129
  50.7 0.0 copy-start.1
  50.8 0.0 copy-start.9
  50.8 2.2 %fusion.40 = (bf16[1,8,160,320]{3,2,1,0:T(8,128)(2,1)S(1)}, bf16[1,8,160,320]{3,2,1,0:T(8,128)(2,1)S(1)}, bf16[1,8,160,320]{3,2,1,0:T(8,128)(2,1)S(1)}) fusion(bf16[3,8,160,320]{3,2,1,0:T(8,128)(2,1)} %get-tuple-element.7), kind=kLoop, calls=%fused_computation.96 | loop fusion | bytes 4915200 | tf_op jit(solution)/shard_map/slice | solution.py:194
  52.9 0.0 copy-done.1
  52.9 0.2 multiply_reduce_fusion
  53.2 0.0 copy-done.9
  53.2 0.6 convolution_convert_fusion.4
  53.8 0.0 copy-start.8
  53.8 0.6 convolution_convert_fusion.3
  54.4 0.0 copy-done.8
  54.4 0.1 select_reduce_fusion
  54.5 0.1 broadcast_compare_fusion
  54.6 0.3 fusion.3
  55.0 0.5 fusion.42
  55.5 0.6 convolution_convert_fusion.5
  56.1 0.0 copy-start.2
  56.1 0.4 convolution_convert_fusion.2
  56.5 0.9 copy-done.2
  57.5 0.8 copy.29
  58.2 1.4 %convolution_convert_fusion = bf16[256,1280]{1,0:T(8,128)(2,1)} fusion(bf16[256,320]{0,1:T(8,128)(2,1)S(1)} %bitcast.134, bf16[320,1280]{0,1:T(8,128)(2,1)S(1)} %bitcast.117), kind=kOutput, calls=%fused_computation.1 | convolution fusion | flops 210042880 | bytes 1638400 | tf_op jit(solution)/shard_map/dot_general | solution.py:204
  59.6 11.0 %exchange_1.1 = bf16[4,64,1280]{2,1,0:T(8,128)(2,1)} custom-call(bf16[4,64,1280]{2,1,0:T(8,128)(2,1)} %bitcast.118), custom_call_target="tpu_custom_call" | custom-call | tf_op jit(solution)/shard_map/exchange_1/pallas_call | solution.py:55
  70.7 1.2 convert_reduce_fusion
  71.9 0.0 copy-start.6
  71.9 0.1 convert_element_type.60
  72.0 0.1 multiply_reduce_fusion.1
  72.2 0.4 copy-done.6
  72.6 0.1 multiply_convert_fusion.1
  72.7 0.1 reshape.363
  72.8 0.7 copy.71
  73.4 9.5 %exchange_2.1.x_ref = bf16[8,16,640]{2,1,0:T(8,128)(2,1)} custom-call(bf16[8,16,640]{2,1,0:T(8,128)(2,1)} %bitcast.131), custom_call_target="tpu_custom_call" | custom-call | tf_op jit(solution)/shard_map/exchange_2/pallas_call | solution.py:55
  82.9 9.8 %exchange_3.1 = bf16[4,8,16,640]{3,2,1,0:T(8,128)(2,1)} custom-call(bf16[8,16,640]{2,1,0:T(8,128)(2,1)} %exchange_2.1.x_ref), custom_call_target="tpu_custom_call" | custom-call | tf_op jit(solution)/shard_map/exchange_3/pallas_call | solution.py:55
  92.7 1.2 copy.31
  93.8 0.0 copy-done.4
  93.9 0.1 copy.52
  94.0 1.4 %convolution_convert_fusion.1 = bf16[512,512]{1,0:T(8,128)(2,1)} fusion(bf16[512,640]{1,0:T(8,128)(2,1)S(1)} %bitcast.129, bf16[640,512]{1,0:T(8,128)(2,1)S(1)} %bitcast.130), kind=kOutput, calls=%fused_computation.9 | convolution fusion | flops 335806464 | bytes 1835008 | tf_op jit(solution)/shard_map/dot_general | solution.py:216
  95.4 15.4 %exchange_4.1 = bf16[8,64,512]{2,1,0:T(8,128)(2,1)} custom-call(bf16[8,64,512]{2,1,0:T(8,128)(2,1)} %bitcast.132), custom_call_target="tpu_custom_call" | custom-call | tf_op jit(solution)/shard_map/exchange_4/pallas_call | solution.py:55
  110.8 0.0 copy-start.10
  110.8 1.8 %reduce_sum.98.x_ref = bf16[64,512]{1,0:T(8,128)(2,1)} reduce(bf16[8,64,512]{2,1,0:T(8,128)(2,1)} %exchange_4.1, bf16[]{:T(256)} %constant.81.clone.1), dimensions={0}, to_apply=%region_6.7 | reduce | flops 229376 | bytes 589826 | tf_op jit(solution)/shard_map/reduce_sum | solution.py:220
  112.5 17.9 %exchange_5.1 = bf16[8,64,512]{2,1,0:T(8,128)(2,1)} custom-call(bf16[64,512]{1,0:T(8,128)(2,1)} %reduce_sum.98.x_ref), custom_call_target="tpu_custom_call" | custom-call | tf_op jit(solution)/shard_map/exchange_5/pallas_call | solution.py:55
  130.4 0.0 copy-start.3
  130.4 0.0 copy-done
  130.4 0.1 constant_dynamic-slice_fusion
  130.5 0.1 compare_and_fusion
  130.6 0.0 copy-done.7
  130.6 1.1 fusion.45
  131.7 0.0 copy-done.5
  131.8 0.1 reshape.375
  131.9 0.2 fusion.41
  132.1 0.1 iota_compare_fusion
  132.1 0.2 fusion.46
  132.3 0.2 fusion.26
  132.5 0.2 fusion.18
  132.7 1.1 fusion.17
  133.8 0.2 fusion.15
  134.0 0.2 fusion.43
  134.2 0.2 fusion.44
  134.4 0.2 fusion.28
  134.6 0.2 fusion.20
  134.8 0.2 fusion.16
  135.0 0.2 fusion.14
  135.2 0.6 copy.72
  (17 shorter events, 0.1 us)
Async XLA Ops:
  0.0 130.4 %copy-start = (s32[16,2]{0,1:T(2,128)S(1)}, s32[16,2]{0,1:T(2,128)}, u32[]{:S(2)}) copy-start(s32[16,2]{0,1:T(2,128)} %param.21) | copy-start | bytes 388
  50.7 2.2 %copy-start.1 = (bf16[256,1280]{1,0:T(8,128)(2,1)S(1)}, bf16[256,1280]{1,0:T(8,128)(2,1)}, u32[]{:S(2)}) copy-start(bf16[256,1280]{1,0:T(8,128)(2,1)} %param.11) | copy-start | bytes 1966084
  50.8 2.4 %copy-start.9 = (f32[1280]{0:T(1024)S(1)}, f32[1280]{0:T(1024)}, u32[]{:S(2)}) copy-start(f32[1280]{0:T(1024)} %param.12) | copy-start | bytes 15364
  53.8 0.7 copy-start.8
  56.1 1.3 copy-start.2
  71.9 0.7 copy-start.6
  73.4 20.4 %copy-start.4 = (bf16[640,2,256]{2,1,0:T(2,128)(2,1)S(1)}, bf16[640,2,256]{2,1,0:T(2,128)(2,1)}, u32[]{:S(2)}) copy-start(bf16[640,2,256]{2,1,0:T(2,128)(2,1)} %param.17) | copy-start | bytes 1966084
  95.4 35.2 %copy-start.7 = (bf16[2,2048]{1,0:T(2,128)(2,1)S(1)}, bf16[2,2048]{1,0:T(2,128)(2,1)}, u32[]{:S(2)}) copy-start(bf16[2,2048]{1,0:T(2,128)(2,1)} %param.18) | copy-start | bytes 24580
  95.4 36.4 %copy-start.5 = (bf16[2,64,2,256]{3,2,1,0:T(2,128)(2,1)S(1)}, bf16[2,64,2,256]{3,2,1,0:T(2,128)(2,1)}, u32[]{:S(2)}) copy-start(bf16[2,64,2,256]{3,2,1,0:T(2,128)(2,1)} %param.19) | copy-start | bytes 393220
  110.8 21.3 %copy-start.10 = (s32[2]{0:T(128)S(1)}, s32[2]{0:T(128)}, u32[]{:S(2)}) copy-start(s32[2]{0:T(128)} %param.20) | copy-start | bytes 28
  130.4 3.6 %copy-start.3 = (bf16[8,64,512]{2,1,0:T(8,128)(2,1)S(1)}, bf16[8,64,512]{2,1,0:T(8,128)(2,1)}, u32[]{:S(2)}) copy-start(bf16[8,64,512]{2,1,0:T(8,128)(2,1)} %exchange_5.1) | copy-start | bytes 1572868
where the time goes:
time: 138 us; the launch traced here: 136 us
  Pallas kernels  113 us (82%)
  matrix products  9.31 us (7%)
  local copies, waits for them, and re-layouts  9.02 us (7%)
  other arithmetic  4.59 us (3%)
    pallas_call x5, Pallas kernels, exchange(): pl.pallas_call(functools.partial(exchange_kernel, axis, count, gather), o...  63.6 us
    pallas_call x1, Pallas kernels, ring_weights(): pl.pallas_call(functools.partial(ring_kernel, count), out_shape=(jax.Shap...  49 us
    unnamed x26, local copies, waits for them, and re-layouts  3.84 us

commit v1 on v0

--- a/solution.py
+++ b/solution.py
@@ -265,6 +265,499 @@
     return jnp.stack(answers, axis=1).reshape(quest_count, -1)
 
 
+def fused_kernel(
+    seq_count,
+    head_count,
+    patches_ref,
+    norm_gain_ref,
+    merge_gain_ref,
+    wq_ref,
+    wo_ref,
+    order_ref,
+    wkv_ref,
+    asks_ref,
+    suffix_ref,
+    lengths_ref,
+    range_ref,
+    out_ref,
+    rows_all,
+    order_all,
+    normed,
+    wq_all,
+    wo_all,
+    wkv_all,
+    asks_all,
+    swap_out,
+    swap_in,
+    core_out,
+    core_in,
+    side_out,
+    side_in,
+    merged_out,
+    merged_all,
+    kv_out,
+    kv_in,
+    mixed_out,
+    mixed_in,
+    level_out,
+    level_in,
+    send_sems,
+    recv_sems,
+):
+    planes = seq_count // 2
+    me = lax.axis_index("seq")
+    head = lax.axis_index("head")
+    z, y = me // 2, lax.rem(me, 2)
+    x, c = head // 2, lax.rem(head, 2)
+    half = lax.rem(z, 2)
+    group = 2 * c + x
+    frame_rows, depth = patches_ref.shape
+    group_rows = frame_rows // head_count
+    share = group_rows // 4
+    head_size = VD // VH
+    own_width = 2 * head_size
+
+    def at(z_to, y_to, x_to, c_to):
+        return {"seq": 2 * z_to + y_to, "head": 2 * x_to + c_to}
+
+    partner = z + 1 - 2 * half
+    across = at(z, 1 - y, x, c)
+    beside = at(z, y, 1 - x, c)
+    twin = at(z, y, x, 1 - c)
+    paired = at(partner, y, x, c)
+
+    def plane_at(step):
+        return lax.rem(z + step, planes)
+
+    def plane_from(step):
+        return lax.rem(z + planes - step, planes)
+
+    barrier = pltpu.get_barrier_semaphore()
+    peers = [
+        {"seq": lax.rem(me + step, seq_count), "head": head} for step in range(1, seq_count)
+    ] + [beside, twin]
+    for peer in peers:
+        pl.semaphore_signal(barrier, inc=1, device_id=peer, device_id_type=MESH)
+
+    copies = {}
+
+    def send(name, src, dst, device):
+        slot = len(copies)
+        copy = pltpu.make_async_remote_copy(
+            src_ref=src,
+            dst_ref=dst,
+            send_sem=send_sems.at[slot],
+            recv_sem=recv_sems.at[slot],
+            device_id=device,
+            device_id_type=MESH,
+        )
+        copy.start()
+        copies[name] = copy
+
+    def arrived(name):
+        copies[name].wait_recv()
+
+    for part in range(head_count):
+        row = lax.broadcasted_iota(jnp.int32, (group_rows, frame_rows), 0)
+        place = lax.broadcasted_iota(jnp.int32, (group_rows, frame_rows), 1)
+        picked = 4 * (share * part + lax.rem(row, share)) + row // share
+        pick = jnp.where(place == picked, 1.0, 0.0).astype(jnp.bfloat16)
+        rows_all[half, pl.ds(part * group_rows, group_rows), :] = jnp.dot(
+            pick, patches_ref[...], preferred_element_type=jnp.float32
+        ).astype(jnp.bfloat16)
+    order_all[half] = order_ref[...]
+    wq_all[me] = wq_ref[half]
+    wo_all[me] = wo_ref[...]
+    wkv_all[y] = wkv_ref[...]
+    asks_all[me] = asks_ref[...]
+    pl.semaphore_wait(barrier, len(peers))
+
+    steps = [1] + ([planes - 1] if planes > 2 else []) + list(range(2, planes - 1))
+    quarter = pl.ds(pl.multiple_of(group * group_rows, group_rows), group_rows)
+    send("order", order_all.at[half], order_all.at[half], paired)
+    send("rows", rows_all.at[half, quarter], rows_all.at[half, quarter], paired)
+    send("wq_y0", wq_ref.at[half], wq_all.at[me], across)
+    for step in steps:
+        to = plane_at(step)
+        send(f"wq_z{step}", wq_ref.at[lax.rem(to, 2)], wq_all.at[me], at(to, y, x, c))
+    send("wo_y0", wo_ref, wo_all.at[me], across)
+    for step in steps:
+        send(f"wo_z{step}", wo_ref, wo_all.at[me], at(plane_at(step), y, x, c))
+    for step in range(1, seq_count):
+        send(
+            f"ask{step}",
+            asks_ref,
+            asks_all.at[me],
+            {"seq": lax.rem(me + step, seq_count), "head": head},
+        )
+
+    def normalise(slot):
+        for part in range(head_count):
+            rows = pl.ds(part * group_rows, group_rows)
+            source = rows_all[slot, rows, :].astype(jnp.float32)
+            normed[slot, rows, :] = rms_scale(source, norm_gain_ref[...]).astype(jnp.bfloat16)
+
+    normalise(half)
+
+    span = suffix_ref.shape[2]
+    kv_heads = asks_ref.shape[0]
+    asking = asks_ref.shape[1] // suffix_ref.shape[0]
+    scale = HD ** (-0.5)
+    tails = []
+    for g in range(kv_heads):
+        columns = slice(g * HD, (g + 1) * HD)
+        mixes, levels = [], []
+        for q in range(suffix_ref.shape[0]):
+            ask = asks_ref[g, q * asking : (q + 1) * asking, :]
+            keys = suffix_ref[q, 0, :, columns]
+            values = suffix_ref[q, 1, :, columns]
+            scores = (
+                lax.dot_general(
+                    ask, keys, (((1,), (1,)), ((), ())), preferred_element_type=jnp.float32
+                )
+                * scale
+            )
+            place = lax.broadcasted_iota(jnp.int32, scores.shape, 1)
+            scores = jnp.where(place < lengths_ref[q], scores, -1e30)
+            highest = jnp.max(scores, axis=1, keepdims=True)
+            weights = jnp.exp(scores - highest)
+            total = jnp.sum(weights, axis=1, keepdims=True)
+            mix = jnp.dot(
+                weights.astype(jnp.bfloat16), values, preferred_element_type=jnp.float32
+            )
+            mixes.append(mix / total)
+            levels.append(highest + jnp.log(total))
+        tails.append((jnp.concatenate(mixes, axis=0), jnp.concatenate(levels, axis=0)))
+
+    def forward(name, ref, index, device):
+        send(name, ref.at[index], ref.at[index], device)
+
+    other = 1 - half
+    arrived("rows")
+    send("rows_x", rows_all.at[other, quarter], rows_all.at[other, quarter], beside)
+    send("rows_c", rows_all.at[other, quarter], rows_all.at[other, quarter], twin)
+    first, second = steps[0], (steps[1] if len(steps) > 1 else None)
+
+    def wq_step(step):
+        arrived(f"wq_z{step}")
+        forward(f"wq_y{step}", wq_all, 2 * plane_from(step) + y, across)
+
+    wq_step(steps[0])
+    arrived("rows_x")
+    side_quarter = pl.ds(
+        pl.multiple_of((2 * c + 1 - x) * group_rows, group_rows), group_rows
+    )
+    send("rows_xc", rows_all.at[other, side_quarter], rows_all.at[other, side_quarter], twin)
+    for step in steps[1:2]:
+        wq_step(step)
+    arrived("rows_c")
+    arrived("rows_xc")
+    arrived("order")
+    normalise(other)
+    for step in steps[2:]:
+        wq_step(step)
+    for step in [0] + steps:
+        arrived(f"wq_y{step}")
+
+    def wo_step(step):
+        arrived(f"wo_z{step}")
+        forward(f"wo_y{step}", wo_all, 2 * plane_from(step) + y, across)
+
+    lane = lax.broadcasted_iota(jnp.int32, (frame_rows, 256), 1)
+
+    def attend(slot):
+        unit_count = order_ref.shape[1]
+        row = lax.broadcasted_iota(jnp.int32, (frame_rows, unit_count), 0)
+        unit = row // group_rows * share + lax.rem(row, share)
+        place = lax.broadcasted_iota(jnp.int32, (frame_rows, unit_count), 1)
+        window = jnp.sum(
+            jnp.where(order_all[slot] == unit, place // (WIN // 4), 0).astype(jnp.float32),
+            axis=1,
+            keepdims=True,
+        )
+        sort = lax.broadcasted_iota(jnp.int32, (frame_rows, 128), 1).astype(jnp.float32)
+        member = jnp.where(window == sort, 1.0, 0.0).astype(jnp.bfloat16)
+        same = (
+            lax.dot_general(
+                member, member, (((1,), (1,)), ((), ())), preferred_element_type=jnp.float32
+            )
+            > 0.5
+        )
+        qkv = jnp.dot(
+            normed[slot],
+            wq_all[...].reshape(depth, wq_ref.shape[2]),
+            preferred_element_type=jnp.float32,
+        )
+        width = qkv.shape[1]
+        query = qkv[:, :256].astype(jnp.bfloat16)
+        key = pltpu.roll(qkv, width - own_width, 1)[:, :256].astype(jnp.bfloat16)
+        value = pltpu.roll(qkv, width - 2 * own_width, 1)[:, :256].astype(jnp.bfloat16)
+        mixed = jnp.zeros((frame_rows, 256), jnp.float32)
+        for i in range(2):
+            inside = (lane >= i * head_size) & (lane < (i + 1) * head_size)
+            scores = lax.dot_general(
+                jnp.where(inside, query, jnp.zeros_like(query)),
+                key,
+                (((1,), (1,)), ((), ())),
+                preferred_element_type=jnp.float32,
+            ) * head_size ** (-0.5)
+            scores = jnp.where(same, scores, -1e30)
+            weights = jnp.exp(scores - jnp.max(scores, axis=1, keepdims=True))
+            weights = weights / jnp.sum(weights, axis=1, keepdims=True)
+            product = jnp.dot(
+                weights.astype(jnp.bfloat16), value, preferred_element_type=jnp.float32
+            )
+            mixed = jnp.where(inside, product, mixed)
+        shifted = pltpu.roll(mixed, own_width - 128, 1)
+        return jnp.where(half == 0, mixed, shifted).astype(jnp.bfloat16)
+
+    swap_out[...] = attend(other)
+    send("swap", swap_out, swap_in, paired)
+    for step in steps:
+        wo_step(step)
+    send("wkv", wkv_ref, wkv_all.at[y], across)
+    mine = attend(half)
+    arrived("swap")
+    theirs = swap_in[...]
+    low = jnp.where(half == 0, mine, theirs)
+    high = jnp.where(half == 0, theirs, mine)
+    attended = jnp.concatenate(
+        [low[:, :128], low[:, 128:] + high[:, :128], high[:, 128:]], axis=1
+    )
+    for step in [0] + steps:
+        arrived(f"wo_y{step}")
+    partial = lax.dot_general(
+        attended,
+        wo_all[...].reshape(depth, wo_ref.shape[1]),
+        (((1,), (1,)), ((), ())),
+        preferred_element_type=jnp.float32,
+    )
+    both = 2 * group_rows
+    top, bottom = partial[:both], partial[both:]
+    core_out[...] = jnp.where(c == 0, bottom, top).astype(jnp.bfloat16)
+    send("core", core_out, core_in, twin)
+    kept = jnp.where(c == 0, top, bottom)
+    arrived("core")
+    kept = kept + core_in[...].astype(jnp.float32)
+    top, bottom = kept[:group_rows], kept[group_rows:]
+    side_out[...] = jnp.where(x == 0, bottom, top).astype(jnp.bfloat16)
+    send("side", side_out, side_in, beside)
+    kept = jnp.where(x == 0, top, bottom) + rows_all[half, quarter, :].astype(jnp.float32)
+    arrived("side")
+    hidden = kept + side_in[...].astype(jnp.float32)
+    merged = rms_scale(hidden, merge_gain_ref[...]).astype(jnp.bfloat16)
+    merged_out[...] = merged.reshape(planes, share, depth)
+
+    merged_all[z, group] = merged_out[z]
+    send("mx0", merged_out.at[z], merged_all.at[z, group], beside)
+    send("mc0", merged_out.at[z], merged_all.at[z, group], twin)
+    for step in steps:
+        to = plane_at(step)
+        send(f"mz{step}", merged_out.at[to], merged_all.at[z, group], at(to, y, x, c))
+    side_group = 2 * c + 1 - x
+    for step in steps:
+        arrived(f"mz{step}")
+        source = merged_all.at[plane_from(step), group]
+        send(f"mx{step}", source, source, beside)
+        send(f"mc{step}", source, source, twin)
+    for step in [0] + steps:
+        arrived(f"mx{step}")
+        source = merged_all.at[plane_from(step), side_group]
+        send(f"mxc{step}", source, source, twin)
+    arrived("wkv")
+    for step in [0] + steps:
+        arrived(f"mc{step}")
+        arrived(f"mxc{step}")
+    frame_tokens = frame_rows // 4
+    width = wkv_ref.shape[1]
+    weights = wkv_all[...].reshape(depth, width)
+    for step in steps[::-1] + [0]:
+        to = plane_at(step)
+        block = merged_all[to].reshape(frame_tokens, depth)
+        kv_out[step] = jnp.dot(block, weights, preferred_element_type=jnp.float32).astype(
+            jnp.bfloat16
+        )
+        if step:
+            send(f"kv{step}", kv_out.at[step], kv_in.at[step], at(to, y, x, c))
+    visual = kv_out[0].astype(jnp.float32)
+    for step in steps:
+        arrived(f"kv{step}")
+        visual = visual + kv_in[step].astype(jnp.float32)
+    visual = visual.astype(jnp.bfloat16)
+
+    for step in range(1, seq_count):
+        arrived(f"ask{step}")
+    all_rows = seq_count * asks_ref.shape[1]
+    own_rows = asks_ref.shape[1]
+    questions = range_ref.shape[0]
+    seen = jnp.concatenate(
+        [
+            jnp.full(
+                (asking, 1),
+                jnp.where((range_ref[q, 0] <= me) & (me < range_ref[q, 1]), 0.0, -1e30),
+                jnp.float32,
+            )
+            for q in range(questions)
+        ],
+        axis=0,
+    )
+    level_out[...] = jnp.zeros_like(level_out)
+    diagonal = lax.broadcasted_iota(
+        jnp.int32, (all_rows, all_rows), 0
+    ) == lax.broadcasted_iota(jnp.int32, (all_rows, all_rows), 1)
+    for g in range(kv_heads):
+        ask = asks_all[:, g].reshape(all_rows, HD)
+        keys = visual[:, g * HD : (g + 1) * HD]
+        values = visual[:, (kv_heads + g) * HD : (kv_heads + g + 1) * HD]
+        scores = (
+            lax.dot_general(
+                ask, keys, (((1,), (1,)), ((), ())), preferred_element_type=jnp.float32
+            )
+            * scale
+        )
+        highest = jnp.max(scores, axis=1, keepdims=True)
+        weights = jnp.exp(scores - highest)
+        total = jnp.sum(weights, axis=1, keepdims=True)
+        mix = (
+            jnp.dot(weights.astype(jnp.bfloat16), values, preferred_element_type=jnp.float32)
+            / total
+        )
+        level = highest + jnp.log(total) + seen
+        mixed_out[:, g] = mix.astype(jnp.bfloat16).reshape(seq_count, own_rows, HD)
+        level_out[g : g + 1, :] = jnp.sum(
+            jnp.where(diagonal, level, 0.0), axis=0, keepdims=True
+        )
+    mixed_in[me] = mixed_out[me]
+    level_in[me] = level_out[...]
+    for step in range(1, seq_count):
+        to = lax.rem(me + step, seq_count)
+        send(f"mix{step}", mixed_out.at[to], mixed_in.at[me], {"seq": to, "head": head})
+        send(f"level{step}", level_out, level_in.at[me], {"seq": to, "head": head})
+    for step in range(1, seq_count):
+        arrived(f"mix{step}")
+        arrived(f"level{step}")
+    row = lax.broadcasted_iota(jnp.int32, (own_rows, all_rows), 0)
+    place = lax.broadcasted_iota(jnp.int32, (own_rows, all_rows), 1)
+    chosen = place == row + me * own_rows
+    for g in range(kv_heads):
+        mix, level = tails[g]
+        levels = [
+            jnp.sum(jnp.where(chosen, level_in[s, g : g + 1, :], 0.0), axis=1, keepdims=True)
+            for s in range(seq_count)
+        ]
+        highest = level
+        for other_level in levels:
+            highest = jnp.maximum(highest, other_level)
+        share_of = jnp.exp(level - highest)
+        total = share_of
+        answer = share_of * mix
+        for s in range(seq_count):
+            share_of = jnp.exp(levels[s] - highest)
+            total = total + share_of
+            answer = answer + share_of * mixed_in[s, g].astype(jnp.float32)
+        out_ref[g] = (answer / total).astype(jnp.bfloat16)
+    for copy in copies.values():
+        copy.wait_send()
+
+
+def fused(
+    patches,
+    norm_gain,
+    w_qkv,
+    w_out,
+    window_order,
+    merge_gain,
+    w_kv,
+    queries,
+    suffix_kv,
+    question_lengths,
+    frame_range,
+):
+    seq_count, head_count = lax.axis_size("seq"), lax.axis_size("head")
+    planes = seq_count // 2
+    frame_rows, depth = patches.shape
+    rows, _, columns = w_qkv.shape
+    half = columns // 2
+    quest_count = queries.shape[0]
+    kv_columns = w_kv.shape[2]
+    kv_heads = kv_columns // HD
+    bf16 = jnp.bfloat16
+    wq = w_qkv.transpose(1, 0, 2).reshape(3, rows, 2, half).transpose(2, 1, 0, 3)
+    wq = wq.reshape(2, rows, 3 * half)
+    wq_width = -(-3 * half // 128) * 128
+    wq = jnp.pad(wq, ((0, 0), (0, 0), (0, wq_width - 3 * half)))
+    wo_width = -(-columns // 128) * 128
+    wo = jnp.pad(w_out.T, ((0, 0), (0, wo_width - columns)))
+    wkv = w_kv.reshape(w_kv.shape[0], 2 * kv_columns)
+    asks = queries.reshape(quest_count, kv_heads, -1, HD).transpose(1, 0, 2, 3)
+    asking = asks.shape[2]
+    asks = asks.reshape(kv_heads, quest_count * asking, HD)
+    own_rows = quest_count * asking
+    suffix = suffix_kv.transpose(0, 2, 1, 3)
+    group_rows = frame_rows // head_count
+    share = group_rows // 4
+    messages = 160
+    smem = pl.BlockSpec(memory_space=pltpu.SMEM)
+    answers = pl.pallas_call(
+        functools.partial(fused_kernel, seq_count, head_count),
+        out_shape=jax.ShapeDtypeStruct((kv_heads, own_rows, HD), bf16),
+        in_specs=[VMEM] * 9 + [smem] * 2,
+        out_specs=VMEM,
+        scratch_shapes=[
+            pltpu.VMEM((2, frame_rows, depth), bf16),
+            pltpu.VMEM((2,) + window_order.shape, jnp.int32),
+            pltpu.VMEM((2, frame_rows, depth), bf16),
+            pltpu.VMEM((seq_count, rows, wq_width), bf16),
+            pltpu.VMEM((seq_count,) + wo.shape, bf16),
+            pltpu.VMEM((2,) + wkv.shape, bf16),
+            pltpu.VMEM((seq_count,) + asks.shape, bf16),
+            pltpu.VMEM((frame_rows, 256), bf16),
+            pltpu.VMEM((frame_rows, 256), bf16),
+            pltpu.VMEM((2 * group_rows, depth), bf16),
+            pltpu.VMEM((2 * group_rows, depth), bf16),
+            pltpu.VMEM((group_rows, depth), bf16),
+            pltpu.VMEM((group_rows, depth), bf16),
+            pltpu.VMEM((planes, share, depth), bf16),
+            pltpu.VMEM((planes, head_count, share, depth), bf16),
+            pltpu.VMEM((planes, frame_rows // 4, 2 * kv_columns), bf16),
+            pltpu.VMEM((planes, frame_rows // 4, 2 * kv_columns), bf16),
+            pltpu.VMEM((seq_count,) + asks.shape, bf16),
+            pltpu.VMEM((seq_count,) + asks.shape, bf16),
+            pltpu.VMEM((8, seq_count * own_rows), jnp.float32),
+            pltpu.VMEM((seq_count, 8, seq_count * own_rows), jnp.float32),
+            pltpu.SemaphoreType.DMA((messages,)),
+            pltpu.SemaphoreType.DMA((messages,)),
+        ],
+        compiler_params=pltpu.CompilerParams(
+            collective_id=0, has_side_effects=True, vmem_limit_bytes=60 << 20
+        ),
+        name="fused",
+    )(
+        patches,
+        norm_gain.reshape(1, -1),
+        merge_gain.reshape(1, -1),
+        wq,
+        wo,
+        window_order,
+        wkv,
+        asks,
+        suffix,
+        question_lengths,
+        frame_range,
+    )
+    answers = answers.reshape(kv_heads, quest_count, asking, HD).transpose(1, 0, 2, 3)
+    return answers.reshape(quest_count, -1)
+
+
+def device_program(*arguments):
+    patches, _, w_qkv, _, window_order = arguments[:5]
+    paired = lax.axis_size("seq") == 8 and lax.axis_size("head") == 4
+    whole = patches.shape[0] == FPATCH and window_order.shape[0] == 1
+    if paired and whole and w_qkv.shape[0] % 16 == 0:
+        return fused(*arguments)
+    return on_device(*arguments)
+
+
 def solution(mesh):
     placed = (
         P("seq", None),
@@ -280,5 +773,5 @@
         P(),
     )
     return jax.shard_map(
-        on_device, mesh=mesh, in_specs=placed, out_specs=P("seq", "head"), check_vma=False
+        device_program, mesh=mesh, in_specs=placed, out_specs=P("seq", "head"), check_vma=False
     )

time: 138 us -> 89.6 us (0.65); the launches traced: 136 us -> 89.2 us
  Pallas kernels: 113 us -> 76.4 us
  matrix products: 9.31 us -> 0 us
  other arithmetic: 4.59 us -> 0 us
  local copies, waits for them, and re-layouts: 9.02 us -> 12.8 us
    pallas_call x6 -> x1, Pallas kernels: 113 us -> 76.4 us  [fused(): pl.pallas_call(functools.partial(fused_kernel, seq_count, head_count), ou...]
    dot_general x15 -> x0, matrix products: 8.77 us -> none  [the longest x3 1.8 us: on_device(): jnp.dot(normed, qkv_all[part], preferred_element_type=jnp.float32)]
    reshape x3 -> x6, local copies, waits for them, and re-layouts: 0.83 us -> 5.16 us  [the longest x1 1.34 us: fused(): norm_gain.reshape(1, -1)]
    reduce_sum x9 -> x0, other arithmetic: 4.08 us -> none  [the longest x1 1.75 us: on_device(): visual = jnp.sum(parts.astype(jnp.float32), axis=0).astype(jnp.bfloat16)]
    slice x2 -> x0, local copies, waits for them, and re-layouts: 2.34 us -> none  [the longest x1 2.15 us: on_device(): qkv_all[part]]
    pad x0 -> x2, local copies, waits for them, and re-layouts: none -> 2.32 us  [the longest x1 1.56 us: fused(): wo = jnp.pad(w_out.T, ((0, 0), (0, wo_width - columns)))]
    transpose x2 -> x0, local copies, waits for them, and re-layouts: 1.93 us -> none  [the longest x1 1.15 us: on_device(): merged = merged.transpose(1, 0, 2, 3).reshape(-1, depth)]
    unnamed x26 -> x9, local copies, waits for them, and re-layouts: 3.84 us -> 5.31 us
where the time goes in v1:
time: 89.6 us; the launch traced here: 89.2 us
  Pallas kernels  76.4 us (85%)
  local copies, waits for them, and re-layouts  12.8 us (14%)
    pallas_call x1, Pallas kernels, fused(): pl.pallas_call(functools.partial(fused_kernel, seq_count, head_count), ou...  76.4 us
    unnamed x9, local copies, waits for them, and re-layouts  5.31 us

profile of v1, /device:TPU:0, one launch (start us, length us, event | category | flops | bytes accessed | tf_op | source)
XLA Modules:
  0.0 89.2 jit_solution(2850994008387952123)
XLA Ops:
  0.0 0.0 copy-start.1
  0.0 1.3 %reshape.27.norm_gain_ref = f32[1,1280]{1,0:T(1,128)} reshape(f32[1280]{0:T(1024)} %param.12) | data formatting | bytes 10240 | tf_op jit(solution)/shard_map/reshape | solution.py:737
  1.3 1.3 %reshape.28.merge_gain_ref = f32[1,1280]{1,0:T(1,128)} reshape(f32[1280]{0:T(1024)} %param.16) | data formatting | bytes 10240 | tf_op jit(solution)/shard_map/reshape | solution.py:738
  2.6 1.3 %copy_bitcast_fusion.4.asks_ref = bf16[2,16,128]{2,1,0:T(8,128)(2,1)} fusion(bf16[1,2,16,128]{3,1,2,0:T(2,128)(2,1)} %bitcast.36), kind=kLoop, calls=%fused_computation.4 | loop fusion | bytes 16384 | tf_op jit(solution)/shard_map/reshape | solution.py:694
  3.9 1.3 %copy.21.range_ref = s32[16,2]{1,0:T(8,128)} copy(s32[16,2]{0,1:T(2,128)} %param.21) | data formatting | bytes 256 | tf_op args[10]
  5.3 1.6 %pad.9.wo_ref = bf16[160,384]{1,0:T(8,128)(2,1)} pad(bf16[160,320]{1,0:T(8,128)(2,1)} %bitcast.35, bf16[]{:T(256)} %constant.2.clone.1), padding=0_0x0_64 | pad | bytes 225282 | tf_op jit(solution)/shard_map/jit(_pad)/pad | solution.py:690
  6.8 1.6 %copy.32 = bf16[2,64,2,256]{3,1,2,0:T(8,128)(2,1)} copy(bf16[2,64,2,256]{3,2,1,0:T(2,128)(2,1)} %param.19) | data formatting | bytes 262144 | tf_op args[8]
  8.4 0.0 copy-done.1
  8.4 0.2 reshape.29
  8.6 0.9 copy.17
  9.5 0.0 copy-start
  9.5 0.2 copy.18
  9.7 0.8 pad.8.wq_ref
  10.4 0.1 copy-done
  10.6 1.0 %copy.23 = bf16[80,8,2,256]{3,1,2,0:T(8,128)(2,1)} copy(bf16[80,8,2,256]{3,2,1,0:T(2,128)(2,1)S(1)} %bitcast.32) | data formatting | bytes 1310720
  11.5 76.4 %fused.1 = bf16[2,16,128]{2,1,0:T(8,128)(2,1)} custom-call(bf16[256,1280]{1,0:T(8,128)(2,1)} %patches_ref.1, f32[1,1280]{1,0:T(1,128)} %reshape.27.norm_gain_ref, f32[1,1280]{1,0:T(1,128)} %reshape.28.merge_gain_ref, bf16[2,160,512]{2,1,0:T(8,128)(2,1)} %pad.8.wq_ref, bf16[160,384]{1,0:T(8,128)(2,1)} %pad.9.wo_ref, s32[1,64]{1,0:T(1,128)} %order_ref.1, ...), custom_call_target="tpu_custom_call" | custom-call | tf_op jit(solution)/shard_map/fused/pallas_call | solution.py:701
  87.9 0.7 copy_bitcast_fusion.3
  88.6 0.6 copy.33
Async XLA Ops:
  0.0 8.4 %copy-start.1 = (bf16[160,3,320]{2,0,1:T(8,128)(2,1)S(1)}, bf16[160,3,320]{2,0,1:T(8,128)(2,1)}, u32[]{:S(2)}) copy-start(bf16[160,3,320]{2,0,1:T(8,128)(2,1)} %param.13) | copy-start | bytes 921604
  9.5 1.1 %copy-start = (bf16[640,2,256]{2,1,0:T(2,128)(2,1)S(1)}, bf16[640,2,256]{2,1,0:T(2,128)(2,1)}, u32[]{:S(2)}) copy-start(bf16[640,2,256]{2,1,0:T(2,128)(2,1)} %param.17) | copy-start | bytes 1966084

commit v2 on v1

--- a/solution.py
+++ b/solution.py
@@ -271,20 +271,26 @@
     patches_ref,
     norm_gain_ref,
     merge_gain_ref,
-    wq_ref,
+    wqkv_ref,
     wo_ref,
     order_ref,
     wkv_ref,
-    asks_ref,
+    queries_ref,
     suffix_ref,
     lengths_ref,
     range_ref,
     out_ref,
+    wide,
+    wq_ref,
+    kv_ref,
+    asks_ref,
     rows_all,
     order_all,
     normed,
     wq_all,
+    wo_packed,
     wo_all,
+    wo_full,
     wkv_all,
     asks_all,
     swap_out,
@@ -295,8 +301,10 @@
     side_in,
     merged_out,
     merged_all,
-    kv_out,
-    kv_in,
+    key_out,
+    key_in,
+    value_out,
+    value_in,
     mixed_out,
     mixed_in,
     level_out,
@@ -326,11 +334,20 @@
     twin = at(z, y, x, 1 - c)
     paired = at(partner, y, x, c)
 
-    def plane_at(step):
-        return lax.rem(z + step, planes)
-
-    def plane_from(step):
-        return lax.rem(z + planes - step, planes)
+    low = z < planes // 2
+    inner = (z > 0) & (z < planes - 1)
+
+    def target(k):
+        if k and planes > 2:
+            k = k + jnp.where(inner, 3 - 2 * k, 0)
+        return jnp.where(
+            low, lax.rem(z + 1 + k, planes), lax.rem(z - 1 - k + 2 * planes, planes)
+        )
+
+    def source(j):
+        depth_in = jnp.where(low, z, planes - 1 - z)
+        counted = j + jnp.where(j >= depth_in, 1, 0)
+        return jnp.where(low, counted, planes - 1 - counted)
 
     barrier = pltpu.get_barrier_semaphore()
     peers = [
@@ -339,23 +356,50 @@
     for peer in peers:
         pl.semaphore_signal(barrier, inc=1, device_id=peer, device_id_type=MESH)
 
-    copies = {}
-
-    def send(name, src, dst, device):
-        slot = len(copies)
-        copy = pltpu.make_async_remote_copy(
+    taken = []
+    started = []
+    guarded = []
+
+    def slots(count=1):
+        taken.append(count)
+        return sum(taken) - count
+
+    def copy_of(src, dst, device, send_slot, recv_slot):
+        return pltpu.make_async_remote_copy(
             src_ref=src,
             dst_ref=dst,
-            send_sem=send_sems.at[slot],
-            recv_sem=recv_sems.at[slot],
+            send_sem=send_sems.at[send_slot],
+            recv_sem=recv_sems.at[recv_slot],
             device_id=device,
             device_id_type=MESH,
         )
+
+    def send(src, dst, device, send_slot, recv_slot):
+        copy = copy_of(src, dst, device, send_slot, recv_slot)
         copy.start()
-        copies[name] = copy
-
-    def arrived(name):
-        copies[name].wait_recv()
+        started.append(copy)
+        return copy
+
+    def send_if(inside, src, dst, device, send_slot, recv_slot):
+        copy = copy_of(src, dst, device, send_slot, recv_slot)
+
+        @pl.when(inside)
+        def _():
+            copy.start()
+
+        guarded.append((inside, copy))
+
+    def send_all(count, slot, copy_at):
+        for step in range(1, count):
+            src, dst, device = copy_at(step)
+            copy_of(src, dst, device, slot, slot).start()
+
+    def left(copy):
+        started[:] = [kept for kept in started if kept is not copy]
+        copy.wait_send()
+
+    def arrived(ref, slot, name):
+        copy_of(ref, ref, twin, slot, slot).wait_recv()
 
     for part in range(head_count):
         row = lax.broadcasted_iota(jnp.int32, (group_rows, frame_rows), 0)
@@ -365,52 +409,121 @@
         rows_all[half, pl.ds(part * group_rows, group_rows), :] = jnp.dot(
             pick, patches_ref[...], preferred_element_type=jnp.float32
         ).astype(jnp.bfloat16)
+    columns = wqkv_ref.shape[2]
+    wq_width = wq_ref.shape[2]
+    lane = lax.broadcasted_iota(jnp.int32, wq_ref.shape[1:], 1)
+    packed = [jnp.zeros(wq_ref.shape[1:], jnp.float32)] * 2
+    wide[...] = jnp.zeros_like(wide)
+    for part in range(3):
+        wide[part, :, :columns] = wqkv_ref[part].astype(jnp.float32)
+        for side in range(2):
+            shift = (part - side) * own_width
+            moved = wide[part] if shift == 0 else pltpu.roll(wide[part], shift % wq_width, 1)
+            inside = (lane >= part * own_width) & (lane < (part + 1) * own_width)
+            packed[side] = jnp.where(inside, moved, packed[side])
+    for side in range(2):
+        wq_ref[side] = packed[side].astype(jnp.bfloat16)
     order_all[half] = order_ref[...]
+    pl.semaphore_wait(barrier, len(peers))
+
+    quarter = pl.ds(pl.multiple_of(group * group_rows, group_rows), group_rows)
+    far = planes - 1
+    order_slot, rows_slot, rows_x_slot, rows_c_slot, rows_xc_slot = (slots() for _ in range(5))
+    wq_z, wq_y, wo_z, wo_y = (slots(planes) for _ in range(4))
+    send(order_all.at[half], order_all.at[half], paired, order_slot, order_slot)
+
+    def wq_send(k, inside=None):
+        to = target(k)
+        copy = (
+            wq_ref.at[lax.rem(to, 2)],
+            wq_all.at[me],
+            at(to, y, x, c),
+            wq_z + k,
+            wq_z + z,
+        )
+        return send(*copy) if inside is None else send_if(inside, *copy)
+
+    def over_y(ref, plane, base):
+        own = ref.at[2 * plane + y]
+        return send(own, own, across, base + plane, base + plane)
+
+    def hear_y(ref, plane, base, name):
+        arrived(ref.at[2 * plane + 1 - y], base + plane, name)
+
+    def wq_hear(j):
+        plane = source(j)
+        arrived(wq_all.at[2 * plane + y], wq_z + plane, "wq_z")
+        return over_y(wq_all, plane, wq_y)
+
+    outer = jnp.logical_not(inner)
+    wq_first = wq_send(0)
+    wq_send(1, inner)
     wq_all[me] = wq_ref[half]
-    wo_all[me] = wo_ref[...]
-    wkv_all[y] = wkv_ref[...]
+    send(wq_ref.at[half], wq_all.at[me], across, wq_y + z, wq_y + z)
+
+    kv_columns = wkv_ref.shape[2]
+    for side in range(2):
+        kv_ref[:, side * kv_columns : (side + 1) * kv_columns] = wkv_ref[:, side, :]
+    early = kv_ref.shape[0] // 4
+    wkv_slot = slots(2)
+    wkv_parts = (pl.ds(0, early), pl.ds(early, kv_ref.shape[0] - early))
+
+    def wkv_send(i):
+        part = wkv_parts[i]
+        send(kv_ref.at[part], wkv_all.at[y, part], across, wkv_slot + i, wkv_slot + i)
+
+    wkv_send(0)
+    wkv_all[y] = kv_ref[...]
+    for i in range(2):
+        for j in range(2):
+            wo_packed[2 * i + j] = wo_ref[i * 80 : (i + 1) * 80, j * 128 : (j + 1) * 128]
+    wo_packed[4] = jnp.concatenate(
+        [wo_ref[:80, 256:320], wo_ref[80:, 256:320]], axis=1
+    )
+    wo_all[me] = wo_packed[...]
+    asked = queries_ref[...].astype(jnp.float32)
+    quest_count = asked.shape[0]
+    kv_heads = wkv_ref.shape[2] // HD
+    asking = asked.shape[1] // (kv_heads * HD)
+    for g in range(kv_heads):
+        asks_ref[g] = jnp.concatenate(
+            [
+                asked[q : q + 1, (g * asking + j) * HD : (g * asking + j + 1) * HD]
+                for q in range(quest_count)
+                for j in range(asking)
+            ],
+            axis=0,
+        ).astype(jnp.bfloat16)
     asks_all[me] = asks_ref[...]
-    pl.semaphore_wait(barrier, len(peers))
-
-    steps = [1] + ([planes - 1] if planes > 2 else []) + list(range(2, planes - 1))
-    quarter = pl.ds(pl.multiple_of(group * group_rows, group_rows), group_rows)
-    send("order", order_all.at[half], order_all.at[half], paired)
-    send("rows", rows_all.at[half, quarter], rows_all.at[half, quarter], paired)
-    send("wq_y0", wq_ref.at[half], wq_all.at[me], across)
-    for step in steps:
-        to = plane_at(step)
-        send(f"wq_z{step}", wq_ref.at[lax.rem(to, 2)], wq_all.at[me], at(to, y, x, c))
-    send("wo_y0", wo_ref, wo_all.at[me], across)
-    for step in steps:
-        send(f"wo_z{step}", wo_ref, wo_all.at[me], at(plane_at(step), y, x, c))
-    for step in range(1, seq_count):
-        send(
-            f"ask{step}",
-            asks_ref,
-            asks_all.at[me],
-            {"seq": lax.rem(me + step, seq_count), "head": head},
-        )
 
     def normalise(slot):
         for part in range(head_count):
             rows = pl.ds(part * group_rows, group_rows)
             source = rows_all[slot, rows, :].astype(jnp.float32)
-            normed[slot, rows, :] = rms_scale(source, norm_gain_ref[...]).astype(jnp.bfloat16)
+            normed[slot, rows, :] = rms_scale(source, norm_gain_ref[...].reshape(1, -1)).astype(jnp.bfloat16)
 
     normalise(half)
 
-    span = suffix_ref.shape[2]
-    kv_heads = asks_ref.shape[0]
-    asking = asks_ref.shape[1] // suffix_ref.shape[0]
+    left(wq_first)
+    rows_copy = send(
+        rows_all.at[half, quarter], rows_all.at[half, quarter], paired, rows_slot, rows_slot
+    )
+    wq_send(2, inner)
+    wq_send(1, outer)
+    wq_hear(0)
+    over_y(wo_all, z, wo_y)
+    left(rows_copy)
+    wq_send(2, outer)
+
     scale = HD ** (-0.5)
     tails = []
     for g in range(kv_heads):
         columns = slice(g * HD, (g + 1) * HD)
         mixes, levels = [], []
-        for q in range(suffix_ref.shape[0]):
+        for q in range(quest_count):
             ask = asks_ref[g, q * asking : (q + 1) * asking, :]
-            keys = suffix_ref[q, 0, :, columns]
-            values = suffix_ref[q, 1, :, columns]
+            keys = suffix_ref[q, :, 0, columns]
+            values = suffix_ref[q, :, 1, columns]
             scores = (
                 lax.dot_general(
                     ask, keys, (((1,), (1,)), ((), ())), preferred_element_type=jnp.float32
@@ -429,39 +542,63 @@
             levels.append(highest + jnp.log(total))
         tails.append((jnp.concatenate(mixes, axis=0), jnp.concatenate(levels, axis=0)))
 
-    def forward(name, ref, index, device):
-        send(name, ref.at[index], ref.at[index], device)
-
     other = 1 - half
-    arrived("rows")
-    send("rows_x", rows_all.at[other, quarter], rows_all.at[other, quarter], beside)
-    send("rows_c", rows_all.at[other, quarter], rows_all.at[other, quarter], twin)
-    first, second = steps[0], (steps[1] if len(steps) > 1 else None)
-
-    def wq_step(step):
-        arrived(f"wq_z{step}")
-        forward(f"wq_y{step}", wq_all, 2 * plane_from(step) + y, across)
-
-    wq_step(steps[0])
-    arrived("rows_x")
+    wo_slots = slots(far + 2)
+
+    def wo_send(plane, to, count):
+        own = wo_all.at[2 * plane + y]
+        send_if(
+            (to >= 0) & (to < planes), own, own, at(to, y, x, c), wo_slots + count, wo_z + plane
+        )
+
+    theirs = rows_all.at[other, quarter]
+    arrived(theirs, rows_slot, "rows")
+    send(theirs, theirs, beside, rows_x_slot, rows_x_slot)
+    send(theirs, theirs, twin, rows_c_slot, rows_c_slot)
+    wq_hear(1)
+    wo_send(z, z + 1, 0)
+    wo_send(z, z - 1, 1)
+    for j in range(2, far):
+        wq_hear(j)
+
+    def unpack(slice_at):
+        for i in range(2):
+            for j in range(2):
+                wo_full[slice_at, i * 80 : (i + 1) * 80, j * 128 : (j + 1) * 128] = wo_all[
+                    slice_at, 2 * i + j
+                ]
+        last = wo_all[slice_at, 4]
+        wo_full[slice_at, :80, 256:384] = last
+        wo_full[slice_at, 80:, 256:384] = pltpu.roll(last.astype(jnp.float32), 64, 1).astype(
+            jnp.bfloat16
+        )
+
+    def wo_hear(j):
+        plane = source(j)
+        arrived(wo_all.at[2 * plane + y], wo_z + plane, "wo_z")
+        wo_send(plane, jnp.where(plane < z, z + 1, z - 1), 2 + j)
+        over_y(wo_all, plane, wo_y)
+        unpack(2 * plane + y)
+
     side_quarter = pl.ds(
         pl.multiple_of((2 * c + 1 - x) * group_rows, group_rows), group_rows
     )
-    send("rows_xc", rows_all.at[other, side_quarter], rows_all.at[other, side_quarter], twin)
-    for step in steps[1:2]:
-        wq_step(step)
-    arrived("rows_c")
-    arrived("rows_xc")
-    arrived("order")
+    beside_rows = rows_all.at[other, side_quarter]
+    arrived(beside_rows, rows_x_slot, "rows_x")
+    send(beside_rows, beside_rows, twin, rows_xc_slot, rows_xc_slot)
+    twin_quarter = pl.ds(
+        pl.multiple_of((2 * (1 - c) + x) * group_rows, group_rows), group_rows
+    )
+    arrived(rows_all.at[other, twin_quarter], rows_c_slot, "rows_c")
+    arrived(rows_all.at[other, twin_quarter], rows_xc_slot, "rows_xc")
+    arrived(order_all.at[other], order_slot, "order")
     normalise(other)
-    for step in steps[2:]:
-        wq_step(step)
-    for step in [0] + steps:
-        arrived(f"wq_y{step}")
-
-    def wo_step(step):
-        arrived(f"wo_z{step}")
-        forward(f"wo_y{step}", wo_all, 2 * plane_from(step) + y, across)
+    unpack(me)
+    wo_hear(0)
+    for plane in range(planes):
+        hear_y(wq_all, plane, wq_y, "wq_y")
+        if plane == 1:
+            wo_hear(1)
 
     lane = lax.broadcasted_iota(jnp.int32, (frame_rows, 256), 1)
 
@@ -511,90 +648,120 @@
         shifted = pltpu.roll(mixed, own_width - 128, 1)
         return jnp.where(half == 0, mixed, shifted).astype(jnp.bfloat16)
 
+    swap_slot, core_slot, side_slot = (slots() for _ in range(3))
     swap_out[...] = attend(other)
-    send("swap", swap_out, swap_in, paired)
-    for step in steps:
-        wo_step(step)
-    send("wkv", wkv_ref, wkv_all.at[y], across)
+    send(swap_out, swap_in, paired, swap_slot, swap_slot)
+    for j in range(2, far):
+        wo_hear(j)
+    ask_slot, mix_slot, level_slot = (slots() for _ in range(3))
+
+    def owner(step):
+        to = lax.rem(me + step, seq_count)
+        return to, {"seq": to, "head": head}
+
+    send_all(seq_count, ask_slot, lambda step: (asks_ref, asks_all.at[me], owner(step)[1]))
+    others = pl.ds(0, seq_count - 1)
     mine = attend(half)
-    arrived("swap")
+    arrived(swap_in, swap_slot, "swap")
     theirs = swap_in[...]
-    low = jnp.where(half == 0, mine, theirs)
-    high = jnp.where(half == 0, theirs, mine)
+    front = jnp.where(half == 0, mine, theirs)
+    back = jnp.where(half == 0, theirs, mine)
     attended = jnp.concatenate(
-        [low[:, :128], low[:, 128:] + high[:, :128], high[:, 128:]], axis=1
-    )
-    for step in [0] + steps:
-        arrived(f"wo_y{step}")
+        [front[:, :128], front[:, 128:] + back[:, :128], back[:, 128:]], axis=1
+    )
+    for plane in range(planes):
+        hear_y(wo_all, plane, wo_y, "wo_y")
+        unpack(2 * plane + 1 - y)
+    wkv_send(1)
     partial = lax.dot_general(
         attended,
-        wo_all[...].reshape(depth, wo_ref.shape[1]),
+        wo_full[...].reshape(depth, wo_full.shape[2]),
         (((1,), (1,)), ((), ())),
         preferred_element_type=jnp.float32,
     )
     both = 2 * group_rows
     top, bottom = partial[:both], partial[both:]
     core_out[...] = jnp.where(c == 0, bottom, top).astype(jnp.bfloat16)
-    send("core", core_out, core_in, twin)
+    send(core_out, core_in, twin, core_slot, core_slot)
     kept = jnp.where(c == 0, top, bottom)
-    arrived("core")
+    arrived(core_in, core_slot, "core")
     kept = kept + core_in[...].astype(jnp.float32)
     top, bottom = kept[:group_rows], kept[group_rows:]
     side_out[...] = jnp.where(x == 0, bottom, top).astype(jnp.bfloat16)
-    send("side", side_out, side_in, beside)
+    send(side_out, side_in, beside, side_slot, side_slot)
     kept = jnp.where(x == 0, top, bottom) + rows_all[half, quarter, :].astype(jnp.float32)
-    arrived("side")
+    arrived(side_in, side_slot, "side")
     hidden = kept + side_in[...].astype(jnp.float32)
-    merged = rms_scale(hidden, merge_gain_ref[...]).astype(jnp.bfloat16)
+    merged = rms_scale(hidden, merge_gain_ref[...].reshape(1, -1)).astype(jnp.bfloat16)
     merged_out[...] = merged.reshape(planes, share, depth)
 
+    mz, mx, mc, mxc, key_slots, value_slots = (slots(planes) for _ in range(6))
+    for k in range(far):
+        to = target(k)
+        send(merged_out.at[to], merged_all.at[z, group], at(to, y, x, c), mz + k, mz + z)
     merged_all[z, group] = merged_out[z]
-    send("mx0", merged_out.at[z], merged_all.at[z, group], beside)
-    send("mc0", merged_out.at[z], merged_all.at[z, group], twin)
-    for step in steps:
-        to = plane_at(step)
-        send(f"mz{step}", merged_out.at[to], merged_all.at[z, group], at(to, y, x, c))
-    side_group = 2 * c + 1 - x
-    for step in steps:
-        arrived(f"mz{step}")
-        source = merged_all.at[plane_from(step), group]
-        send(f"mx{step}", source, source, beside)
-        send(f"mc{step}", source, source, twin)
-    for step in [0] + steps:
-        arrived(f"mx{step}")
-        source = merged_all.at[plane_from(step), side_group]
-        send(f"mxc{step}", source, source, twin)
-    arrived("wkv")
-    for step in [0] + steps:
-        arrived(f"mc{step}")
-        arrived(f"mxc{step}")
+    side_group, twin_group = 2 * c + 1 - x, 2 * (1 - c) + x
+    cross_group = 2 * (1 - c) + 1 - x
+
+    def spread(plane, block):
+        here = merged_all.at[plane, group]
+        send(block, here, beside, mx + plane, mx + plane)
+        send(block, here, twin, mc + plane, mc + plane)
+
+    def relay(plane):
+        block = merged_all.at[plane, side_group]
+        arrived(block, mx + plane, "mx")
+        send(block, block, twin, mxc + plane, mxc + plane)
+
     frame_tokens = frame_rows // 4
-    width = wkv_ref.shape[1]
-    weights = wkv_all[...].reshape(depth, width)
-    for step in steps[::-1] + [0]:
-        to = plane_at(step)
-        block = merged_all[to].reshape(frame_tokens, depth)
-        kv_out[step] = jnp.dot(block, weights, preferred_element_type=jnp.float32).astype(
-            jnp.bfloat16
-        )
-        if step:
-            send(f"kv{step}", kv_out.at[step], kv_in.at[step], at(to, y, x, c))
-    visual = kv_out[0].astype(jnp.float32)
-    for step in steps:
-        arrived(f"kv{step}")
-        visual = visual + kv_in[step].astype(jnp.float32)
-    visual = visual.astype(jnp.bfloat16)
-
-    for step in range(1, seq_count):
-        arrived(f"ask{step}")
+
+    def project(plane):
+        arrived(merged_all.at[plane, twin_group], mc + plane, "mc")
+        arrived(merged_all.at[plane, cross_group], mxc + plane, "mxc")
+        block = merged_all[plane].reshape(frame_tokens, depth)
+        weights = wkv_all[...].reshape(depth, kv_ref.shape[1])
+        return jnp.dot(block, weights, preferred_element_type=jnp.float32)
+
+    def project_to(plane):
+        product = project(plane)
+        key_out[plane] = product[:, :kv_columns]
+        value_out[plane] = product[:, kv_columns:].astype(jnp.bfloat16)
+        to = at(plane, y, x, c)
+        send(key_out.at[plane], key_in.at[z], to, key_slots + plane, key_slots + z)
+        send(value_out.at[plane], value_in.at[z], to, value_slots + plane, value_slots + z)
+
+    planes_heard = [source(j) for j in range(far)]
+    spread(z, merged_out.at[z])
+    for j in range(far):
+        plane = planes_heard[j]
+        arrived(merged_all.at[plane, group], mz + plane, "mz")
+        spread(plane, merged_all.at[plane, group])
+        relay(planes_heard[j - 1] if j else z)
+    for i in range(2):
+        arrived(wkv_all.at[1 - y, wkv_parts[i]], wkv_slot + i, "wkv")
+    for plane in planes_heard[:-2]:
+        project_to(plane)
+    relay(planes_heard[-1])
+    for plane in planes_heard[-2:]:
+        project_to(plane)
+    visual = project(z)
+    keys, values = visual[:, :kv_columns], visual[:, kv_columns:]
+    for plane in planes_heard:
+        arrived(key_in.at[plane], key_slots + plane, "key")
+        arrived(value_in.at[plane], value_slots + plane, "value")
+        keys = keys + key_in[plane]
+        values = values + value_in[plane].astype(jnp.float32)
+    all_keys, all_values = keys.astype(jnp.bfloat16), values.astype(jnp.bfloat16)
+
+    arrived(asks_all.at[others], ask_slot, "ask")
     all_rows = seq_count * asks_ref.shape[1]
     own_rows = asks_ref.shape[1]
-    questions = range_ref.shape[0]
+    questions = range_ref.shape[1]
     seen = jnp.concatenate(
         [
             jnp.full(
                 (asking, 1),
-                jnp.where((range_ref[q, 0] <= me) & (me < range_ref[q, 1]), 0.0, -1e30),
+                jnp.where((range_ref[0, q] <= me) & (me < range_ref[1, q]), 0.0, -1e30),
                 jnp.float32,
             )
             for q in range(questions)
@@ -607,8 +774,8 @@
     ) == lax.broadcasted_iota(jnp.int32, (all_rows, all_rows), 1)
     for g in range(kv_heads):
         ask = asks_all[:, g].reshape(all_rows, HD)
-        keys = visual[:, g * HD : (g + 1) * HD]
-        values = visual[:, (kv_heads + g) * HD : (kv_heads + g + 1) * HD]
+        keys = all_keys[:, g * HD : (g + 1) * HD]
+        values = all_values[:, g * HD : (g + 1) * HD]
         scores = (
             lax.dot_general(
                 ask, keys, (((1,), (1,)), ((), ())), preferred_element_type=jnp.float32
@@ -629,16 +796,18 @@
         )
     mixed_in[me] = mixed_out[me]
     level_in[me] = level_out[...]
-    for step in range(1, seq_count):
-        to = lax.rem(me + step, seq_count)
-        send(f"mix{step}", mixed_out.at[to], mixed_in.at[me], {"seq": to, "head": head})
-        send(f"level{step}", level_out, level_in.at[me], {"seq": to, "head": head})
-    for step in range(1, seq_count):
-        arrived(f"mix{step}")
-        arrived(f"level{step}")
+    send_all(
+        seq_count,
+        mix_slot,
+        lambda step: (mixed_out.at[owner(step)[0]], mixed_in.at[me], owner(step)[1]),
+    )
+    send_all(seq_count, level_slot, lambda step: (level_out, level_in.at[me], owner(step)[1]))
+    arrived(mixed_in.at[others], mix_slot, "mix")
+    arrived(level_in.at[others], level_slot, "level")
     row = lax.broadcasted_iota(jnp.int32, (own_rows, all_rows), 0)
     place = lax.broadcasted_iota(jnp.int32, (own_rows, all_rows), 1)
     chosen = place == row + me * own_rows
+    answers = []
     for g in range(kv_heads):
         mix, level = tails[g]
         levels = [
@@ -655,9 +824,34 @@
             share_of = jnp.exp(levels[s] - highest)
             total = total + share_of
             answer = answer + share_of * mixed_in[s, g].astype(jnp.float32)
-        out_ref[g] = (answer / total).astype(jnp.bfloat16)
-    for copy in copies.values():
+        answers.append(answer / total)
+    out_ref[...] = jnp.concatenate(
+        [
+            jnp.concatenate(
+                [
+                    answers[g][q * asking + j : q * asking + j + 1]
+                    for g in range(kv_heads)
+                    for j in range(asking)
+                ],
+                axis=1,
+            )
+            for q in range(quest_count)
+        ],
+        axis=0,
+    ).astype(jnp.bfloat16)
+    for copy in started:
         copy.wait_send()
+    for block, slot in (
+        (asks_all.at[others], ask_slot),
+        (mixed_in.at[others], mix_slot),
+        (level_in.at[others], level_slot),
+    ):
+        copy_of(block, block, twin, slot, slot).wait_send()
+    for inside, copy in guarded:
+
+        @pl.when(inside)
+        def _(copy=copy):
+            copy.wait_send()
 
 
 def fused(
@@ -678,39 +872,35 @@
     frame_rows, depth = patches.shape
     rows, _, columns = w_qkv.shape
     half = columns // 2
-    quest_count = queries.shape[0]
     kv_columns = w_kv.shape[2]
     kv_heads = kv_columns // HD
     bf16 = jnp.bfloat16
-    wq = w_qkv.transpose(1, 0, 2).reshape(3, rows, 2, half).transpose(2, 1, 0, 3)
-    wq = wq.reshape(2, rows, 3 * half)
     wq_width = -(-3 * half // 128) * 128
-    wq = jnp.pad(wq, ((0, 0), (0, 0), (0, wq_width - 3 * half)))
-    wo_width = -(-columns // 128) * 128
-    wo = jnp.pad(w_out.T, ((0, 0), (0, wo_width - columns)))
-    wkv = w_kv.reshape(w_kv.shape[0], 2 * kv_columns)
-    asks = queries.reshape(quest_count, kv_heads, -1, HD).transpose(1, 0, 2, 3)
-    asking = asks.shape[2]
-    asks = asks.reshape(kv_heads, quest_count * asking, HD)
-    own_rows = quest_count * asking
-    suffix = suffix_kv.transpose(0, 2, 1, 3)
+    asks_shape = (kv_heads, queries.size // (kv_heads * HD), HD)
+    own_rows = asks_shape[1]
     group_rows = frame_rows // head_count
     share = group_rows // 4
-    messages = 160
+    messages = 14 + 11 * (seq_count // 2)
     smem = pl.BlockSpec(memory_space=pltpu.SMEM)
     answers = pl.pallas_call(
         functools.partial(fused_kernel, seq_count, head_count),
-        out_shape=jax.ShapeDtypeStruct((kv_heads, own_rows, HD), bf16),
+        out_shape=jax.ShapeDtypeStruct(queries.shape, bf16),
         in_specs=[VMEM] * 9 + [smem] * 2,
         out_specs=VMEM,
         scratch_shapes=[
+            pltpu.VMEM((3, rows, wq_width), jnp.float32),
+            pltpu.VMEM((2, rows, wq_width), bf16),
+            pltpu.VMEM((w_kv.shape[0], 2 * kv_columns), bf16),
+            pltpu.VMEM(asks_shape, bf16),
             pltpu.VMEM((2, frame_rows, depth), bf16),
             pltpu.VMEM((2,) + window_order.shape, jnp.int32),
             pltpu.VMEM((2, frame_rows, depth), bf16),
             pltpu.VMEM((seq_count, rows, wq_width), bf16),
-            pltpu.VMEM((seq_count,) + wo.shape, bf16),
-            pltpu.VMEM((2,) + wkv.shape, bf16),
-            pltpu.VMEM((seq_count,) + asks.shape, bf16),
+            pltpu.VMEM((5, 80, 128), bf16),
+            pltpu.VMEM((seq_count, 5, 80, 128), bf16),
+            pltpu.VMEM((seq_count, rows, 384), bf16),
+            pltpu.VMEM((2, w_kv.shape[0], 2 * kv_columns), bf16),
+            pltpu.VMEM((seq_count,) + asks_shape, bf16),
             pltpu.VMEM((frame_rows, 256), bf16),
             pltpu.VMEM((frame_rows, 256), bf16),
             pltpu.VMEM((2 * group_rows, depth), bf16),
@@ -719,10 +909,12 @@
             pltpu.VMEM((group_rows, depth), bf16),
             pltpu.VMEM((planes, share, depth), bf16),
             pltpu.VMEM((planes, head_count, share, depth), bf16),
-            pltpu.VMEM((planes, frame_rows // 4, 2 * kv_columns), bf16),
-            pltpu.VMEM((planes, frame_rows // 4, 2 * kv_columns), bf16),
-            pltpu.VMEM((seq_count,) + asks.shape, bf16),
-            pltpu.VMEM((seq_count,) + asks.shape, bf16),
+            pltpu.VMEM((planes, frame_rows // 4, kv_columns), jnp.float32),
+            pltpu.VMEM((planes, frame_rows // 4, kv_columns), jnp.float32),
+            pltpu.VMEM((planes, frame_rows // 4, kv_columns), bf16),
+            pltpu.VMEM((planes, frame_rows // 4, kv_columns), bf16),
+            pltpu.VMEM((seq_count,) + asks_shape, bf16),
+            pltpu.VMEM((seq_count,) + asks_shape, bf16),
             pltpu.VMEM((8, seq_count * own_rows), jnp.float32),
             pltpu.VMEM((seq_count, 8, seq_count * own_rows), jnp.float32),
             pltpu.SemaphoreType.DMA((messages,)),
@@ -734,19 +926,18 @@
         name="fused",
     )(
         patches,
-        norm_gain.reshape(1, -1),
-        merge_gain.reshape(1, -1),
-        wq,
-        wo,
+        norm_gain,
+        merge_gain,
+        w_qkv.transpose(1, 0, 2),
+        w_out.T,
         window_order,
-        wkv,
-        asks,
-        suffix,
+        w_kv,
+        queries,
+        suffix_kv,
         question_lengths,
-        frame_range,
-    )
-    answers = answers.reshape(kv_heads, quest_count, asking, HD).transpose(1, 0, 2, 3)
-    return answers.reshape(quest_count, -1)
+        frame_range.T,
+    )
+    return answers
 
 
 def device_program(*arguments):

time: 89.6 us -> 75.5 us (0.84)
  local copies, waits for them, and re-layouts: 12.8 us -> 1.3 us
  Pallas kernels: 76.4 us -> 74 us
    reshape x6 -> x0, local copies, waits for them, and re-layouts: 5.16 us -> none  [the longest x1 1.34 us: fused(): norm_gain.reshape(1, -1)]
    unnamed x9 -> x1, local copies, waits for them, and re-layouts: 5.31 us -> 1.3 us
    pallas_call x1, Pallas kernels: 76.4 us -> 74 us  [fused(): pl.pallas_call(functools.partial(fused_kernel, seq_count, head_count), ou...]
    pad x2 -> x0, local copies, waits for them, and re-layouts: 2.32 us -> none  [the longest x1 1.56 us: fused(): wo = jnp.pad(w_out.T, ((0, 0), (0, wo_width - columns)))]
where the time goes in v2:
time: 75.5 us; the launch traced here: 75.3 us
  Pallas kernels  74 us (98%)
  local copies, waits for them, and re-layouts  1.3 us (2%)
    pallas_call x1, Pallas kernels, fused(): pl.pallas_call(functools.partial(fused_kernel, seq_count, head_count), ou...  74 us

profile of v2, /device:TPU:0, one launch (start us, length us, event | category | flops | bytes accessed | tf_op | source)
XLA Modules:
  0.0 75.3 jit_solution(1312099720250835548)
XLA Ops:
  0.0 74.0 %fused.1 = bf16[2,2048]{1,0:T(2,128)(2,1)} custom-call(bf16[256,1280]{1,0:T(8,128)(2,1)} %patches_ref.1, f32[1280]{0:T(1024)} %norm_gain_ref.1, f32[1280]{0:T(1024)} %merge_gain_ref.1, bf16[3,160,320]{2,1,0:T(8,128)(2,1)} %bitcast.3, bf16[160,320]{1,0:T(8,128)(2,1)} %bitcast.4, s32[1,64]{1,0:T(1,128)} %order_ref.1, bf16[640,2,256]{2,1,0:T(2,128)(2,1)} %wkv_ref.1, ...), custom_call_target="tpu_custom_call" | custom-call | tf_op jit(solution)/shard_map/fused/pallas_call | solution.py:885
  74.0 1.3 %copy.13 = bf16[2,2048]{1,0:T(2,128)(2,1)} copy(bf16[2,2048]{1,0:T(2,128)(2,1)} %fused.1) | data formatting | bytes 16384

commit v3 on v2

--- a/solution.py
+++ b/solution.py
@@ -268,6 +268,18 @@
 def fused_kernel(
     seq_count,
     head_count,
+    patches_in,
+    norm_gain_in,
+    merge_gain_in,
+    wqkv_in,
+    wo_in,
+    order_in,
+    wkv_in,
+    queries_in,
+    suffix_in,
+    lengths_in,
+    range_in,
+    out_ref,
     patches_ref,
     norm_gain_ref,
     merge_gain_ref,
@@ -279,7 +291,6 @@
     suffix_ref,
     lengths_ref,
     range_ref,
-    out_ref,
     wide,
     wq_ref,
     kv_ref,
@@ -309,6 +320,7 @@
     mixed_in,
     level_out,
     level_in,
+    load_sems,
     send_sems,
     recv_sems,
 ):
@@ -337,17 +349,15 @@
     low = z < planes // 2
     inner = (z > 0) & (z < planes - 1)
 
+    def ordered(outer_plane, inner_plane):
+        plane = jnp.where(inner, inner_plane, outer_plane)
+        return jnp.where(low, plane, planes - 1 - plane)
+
     def target(k):
-        if k and planes > 2:
-            k = k + jnp.where(inner, 3 - 2 * k, 0)
-        return jnp.where(
-            low, lax.rem(z + 1 + k, planes), lax.rem(z - 1 - k + 2 * planes, planes)
-        )
+        return ordered((3, 2, 1)[k], (2, 0, 3)[k])
 
     def source(j):
-        depth_in = jnp.where(low, z, planes - 1 - z)
-        counted = j + jnp.where(j >= depth_in, 1, 0)
-        return jnp.where(low, counted, planes - 1 - counted)
+        return ordered((1, 3, 2)[j], (2, 3, 0)[j])
 
     barrier = pltpu.get_barrier_semaphore()
     peers = [
@@ -356,6 +366,24 @@
     for peer in peers:
         pl.semaphore_signal(barrier, inc=1, device_id=peer, device_id_type=MESH)
 
+    pairs = (
+        (wqkv_in, wqkv_ref),
+        (patches_in, patches_ref),
+        (order_in, order_ref),
+        (norm_gain_in, norm_gain_ref),
+        (wo_in, wo_ref),
+        (wkv_in, wkv_ref),
+        (queries_in, queries_ref),
+        (suffix_in, suffix_ref),
+        (lengths_in, lengths_ref),
+        (merge_gain_in, merge_gain_ref),
+        (range_in, range_ref),
+    )
+    loads = [
+        pltpu.make_async_copy(src, dst, load_sems.at[i]) for i, (src, dst) in enumerate(pairs)
+    ]
+    for load in loads:
+        load.start()
     taken = []
     started = []
     guarded = []
@@ -400,6 +428,9 @@
 
     def arrived(ref, slot, name):
         copy_of(ref, ref, twin, slot, slot).wait_recv()
+
+    for load in loads[:3]:
+        load.wait()
 
     for part in range(head_count):
         row = lax.broadcasted_iota(jnp.int32, (group_rows, frame_rows), 0)
@@ -461,6 +492,8 @@
     wq_all[me] = wq_ref[half]
     send(wq_ref.at[half], wq_all.at[me], across, wq_y + z, wq_y + z)
 
+    for load in loads[3:]:
+        load.wait()
     kv_columns = wkv_ref.shape[2]
     for side in range(2):
         kv_ref[:, side * kv_columns : (side + 1) * kv_columns] = wkv_ref[:, side, :]
@@ -543,23 +576,19 @@
         tails.append((jnp.concatenate(mixes, axis=0), jnp.concatenate(levels, axis=0)))
 
     other = 1 - half
-    wo_slots = slots(far + 2)
-
-    def wo_send(plane, to, count):
-        own = wo_all.at[2 * plane + y]
-        send_if(
-            (to >= 0) & (to < planes), own, own, at(to, y, x, c), wo_slots + count, wo_z + plane
-        )
+    def wo_send(k):
+        send(wo_packed, wo_all.at[me], at(target(k), y, x, c), wo_z + k, wo_z + z)
 
     theirs = rows_all.at[other, quarter]
     arrived(theirs, rows_slot, "rows")
     send(theirs, theirs, beside, rows_x_slot, rows_x_slot)
     send(theirs, theirs, twin, rows_c_slot, rows_c_slot)
     wq_hear(1)
-    wo_send(z, z + 1, 0)
-    wo_send(z, z - 1, 1)
+    for k in range(far - 1):
+        wo_send(k)
     for j in range(2, far):
         wq_hear(j)
+    wo_send(far - 1)
 
     def unpack(slice_at):
         for i in range(2):
@@ -573,12 +602,25 @@
             jnp.bfloat16
         )
 
-    def wo_hear(j):
+    wo_relays = {}
+
+    def wo_hear(j, inside=None):
         plane = source(j)
-        arrived(wo_all.at[2 * plane + y], wo_z + plane, "wo_z")
-        wo_send(plane, jnp.where(plane < z, z + 1, z - 1), 2 + j)
-        over_y(wo_all, plane, wo_y)
-        unpack(2 * plane + y)
+        own = wo_all.at[2 * plane + y]
+        if j not in wo_relays:
+            wo_relays[j] = copy_of(own, own, across, wo_y + plane, wo_y + plane)
+            started.append(wo_relays[j])
+        copy = wo_relays[j]
+
+        def take():
+            arrived(own, wo_z + plane, "wo_z")
+            copy.start()
+            unpack(2 * plane + y)
+
+        if inside is None:
+            take()
+        else:
+            pl.when(inside)(take)
 
     side_quarter = pl.ds(
         pl.multiple_of((2 * c + 1 - x) * group_rows, group_rows), group_rows
@@ -594,11 +636,11 @@
     arrived(order_all.at[other], order_slot, "order")
     normalise(other)
     unpack(me)
-    wo_hear(0)
+    wo_hear(0, outer)
     for plane in range(planes):
         hear_y(wq_all, plane, wq_y, "wq_y")
         if plane == 1:
-            wo_hear(1)
+            wo_hear(1, outer)
 
     lane = lax.broadcasted_iota(jnp.int32, (frame_rows, 256), 1)
 
@@ -651,6 +693,8 @@
     swap_slot, core_slot, side_slot = (slots() for _ in range(3))
     swap_out[...] = attend(other)
     send(swap_out, swap_in, paired, swap_slot, swap_slot)
+    for j in range(2):
+        wo_hear(j, inner)
     for j in range(2, far):
         wo_hear(j)
     ask_slot, mix_slot, level_slot = (slots() for _ in range(3))
@@ -672,7 +716,6 @@
     for plane in range(planes):
         hear_y(wo_all, plane, wo_y, "wo_y")
         unpack(2 * plane + 1 - y)
-    wkv_send(1)
     partial = lax.dot_general(
         attended,
         wo_full[...].reshape(depth, wo_full.shape[2]),
@@ -685,6 +728,7 @@
     send(core_out, core_in, twin, core_slot, core_slot)
     kept = jnp.where(c == 0, top, bottom)
     arrived(core_in, core_slot, "core")
+    wkv_send(1)
     kept = kept + core_in[...].astype(jnp.float32)
     top, bottom = kept[:group_rows], kept[group_rows:]
     side_out[...] = jnp.where(x == 0, bottom, top).astype(jnp.bfloat16)
@@ -739,11 +783,10 @@
         relay(planes_heard[j - 1] if j else z)
     for i in range(2):
         arrived(wkv_all.at[1 - y, wkv_parts[i]], wkv_slot + i, "wkv")
-    for plane in planes_heard[:-2]:
+    for plane in planes_heard[:-1]:
         project_to(plane)
     relay(planes_heard[-1])
-    for plane in planes_heard[-2:]:
-        project_to(plane)
+    project_to(planes_heard[-1])
     visual = project(z)
     keys, values = visual[:, :kv_columns], visual[:, kv_columns:]
     for plane in planes_heard:
@@ -880,14 +923,28 @@
     own_rows = asks_shape[1]
     group_rows = frame_rows // head_count
     share = group_rows // 4
-    messages = 14 + 11 * (seq_count // 2)
-    smem = pl.BlockSpec(memory_space=pltpu.SMEM)
+    messages = 9 + 11 * (seq_count // 2)
+    arguments = (
+        patches,
+        norm_gain,
+        merge_gain,
+        w_qkv.transpose(1, 0, 2),
+        w_out.T,
+        window_order,
+        w_kv,
+        queries,
+        suffix_kv,
+        question_lengths,
+        frame_range.T,
+    )
     answers = pl.pallas_call(
         functools.partial(fused_kernel, seq_count, head_count),
-        out_shape=jax.ShapeDtypeStruct(queries.shape, bf16),
-        in_specs=[VMEM] * 9 + [smem] * 2,
+        out_shape=pltpu.VMEM(queries.shape, bf16),
+        in_specs=[pl.BlockSpec(memory_space=pl.ANY)] * len(arguments),
         out_specs=VMEM,
-        scratch_shapes=[
+        scratch_shapes=[pltpu.VMEM(array.shape, array.dtype) for array in arguments[:-2]]
+        + [pltpu.SMEM(array.shape, array.dtype) for array in arguments[-2:]]
+        + [
             pltpu.VMEM((3, rows, wq_width), jnp.float32),
             pltpu.VMEM((2, rows, wq_width), bf16),
             pltpu.VMEM((w_kv.shape[0], 2 * kv_columns), bf16),
@@ -917,6 +974,7 @@
             pltpu.VMEM((seq_count,) + asks_shape, bf16),
             pltpu.VMEM((8, seq_count * own_rows), jnp.float32),
             pltpu.VMEM((seq_count, 8, seq_count * own_rows), jnp.float32),
+            pltpu.SemaphoreType.DMA((len(arguments),)),
             pltpu.SemaphoreType.DMA((messages,)),
             pltpu.SemaphoreType.DMA((messages,)),
         ],
@@ -924,19 +982,7 @@
             collective_id=0, has_side_effects=True, vmem_limit_bytes=60 << 20
         ),
         name="fused",
-    )(
-        patches,
-        norm_gain,
-        merge_gain,
-        w_qkv.transpose(1, 0, 2),
-        w_out.T,
-        window_order,
-        w_kv,
-        queries,
-        suffix_kv,
-        question_lengths,
-        frame_range.T,
-    )
+    )(*arguments)
     return answers
 
 

time: 75.5 us -> 71.3 us (0.944)
  Pallas kernels: 74 us -> 70.5 us
    pallas_call x1, Pallas kernels: 74 us -> 70.5 us  [fused(): pl.pallas_call(functools.partial(fused_kernel, seq_count, head_count), ou...]
where the time goes in v3:
time: 71.3 us; the launch traced here: 71.1 us
  Pallas kernels  70.5 us (99%)
    pallas_call x1, Pallas kernels, fused(): pl.pallas_call(functools.partial(fused_kernel, seq_count, head_count), ou...  70.5 us

profile of v3, /device:TPU:0, one launch (start us, length us, event | category | flops | bytes accessed | tf_op | source)
XLA Modules:
  0.0 71.1 jit_solution(17004590860030100102)
XLA Ops:
  0.0 70.5 %fused.1 = bf16[2,2048]{1,0:T(2,128)(2,1)S(1)} custom-call(bf16[256,1280]{1,0:T(8,128)(2,1)} %patches_in.1, f32[1280]{0:T(1024)} %norm_gain_in.1, f32[1280]{0:T(1024)} %merge_gain_in.1, bf16[3,160,320]{2,1,0:T(8,128)(2,1)} %bitcast.3, bf16[160,320]{1,0:T(8,128)(2,1)} %bitcast.4, s32[1,64]{1,0:T(1,128)} %order_in.1, bf16[640,2,256]{2,1,0:T(2,128)(2,1)} %wkv_in.1, ...), custom_call_target="tpu_custom_call" | custom-call | tf_op jit(solution)/shard_map/fused/pallas_call | solution.py:940
  70.5 0.6 copy.13

commit v4 on v3

--- a/solution.py
+++ b/solution.py
@@ -636,7 +636,7 @@
     arrived(order_all.at[other], order_slot, "order")
     normalise(other)
     unpack(me)
-    wo_hear(0, outer)
+    wo_hear(0)
     for plane in range(planes):
         hear_y(wq_all, plane, wq_y, "wq_y")
         if plane == 1:
@@ -690,11 +690,10 @@
         shifted = pltpu.roll(mixed, own_width - 128, 1)
         return jnp.where(half == 0, mixed, shifted).astype(jnp.bfloat16)
 
-    swap_slot, core_slot, side_slot = (slots() for _ in range(3))
+    swap_slot, core_slot, side_slot = slots(), slots(2), slots(2)
     swap_out[...] = attend(other)
     send(swap_out, swap_in, paired, swap_slot, swap_slot)
-    for j in range(2):
-        wo_hear(j, inner)
+    wo_hear(1, inner)
     for j in range(2, far):
         wo_hear(j)
     ask_slot, mix_slot, level_slot = (slots() for _ in range(3))
@@ -716,26 +715,32 @@
     for plane in range(planes):
         hear_y(wo_all, plane, wo_y, "wo_y")
         unpack(2 * plane + 1 - y)
-    partial = lax.dot_general(
-        attended,
-        wo_full[...].reshape(depth, wo_full.shape[2]),
-        (((1,), (1,)), ((), ())),
-        preferred_element_type=jnp.float32,
-    )
     both = 2 * group_rows
-    top, bottom = partial[:both], partial[both:]
-    core_out[...] = jnp.where(c == 0, bottom, top).astype(jnp.bfloat16)
-    send(core_out, core_in, twin, core_slot, core_slot)
-    kept = jnp.where(c == 0, top, bottom)
-    arrived(core_in, core_slot, "core")
+    kept = []
+    for i in range(2):
+        part = wo_full[i * (seq_count // 2) : (i + 1) * (seq_count // 2)]
+        partial = lax.dot_general(
+            attended,
+            part.reshape(depth // 2, wo_full.shape[2]),
+            (((1,), (1,)), ((), ())),
+            preferred_element_type=jnp.float32,
+        )
+        top, bottom = partial[:both], partial[both:]
+        core_out[i] = jnp.where(c == 0, bottom, top).astype(jnp.bfloat16)
+        send(core_out.at[i], core_in.at[i], twin, core_slot + i, core_slot + i)
+        kept.append(jnp.where(c == 0, top, bottom))
+    for i in range(2):
+        arrived(core_in.at[i], core_slot + i, "core")
+        total = kept[i] + core_in[i].astype(jnp.float32)
+        top, bottom = total[:group_rows], total[group_rows:]
+        side_out[i] = jnp.where(x == 0, bottom, top).astype(jnp.bfloat16)
+        send(side_out.at[i], side_in.at[i], beside, side_slot + i, side_slot + i)
+        kept[i] = jnp.where(x == 0, top, bottom)
     wkv_send(1)
-    kept = kept + core_in[...].astype(jnp.float32)
-    top, bottom = kept[:group_rows], kept[group_rows:]
-    side_out[...] = jnp.where(x == 0, bottom, top).astype(jnp.bfloat16)
-    send(side_out, side_in, beside, side_slot, side_slot)
-    kept = jnp.where(x == 0, top, bottom) + rows_all[half, quarter, :].astype(jnp.float32)
-    arrived(side_in, side_slot, "side")
-    hidden = kept + side_in[...].astype(jnp.float32)
+    for i in range(2):
+        arrived(side_in.at[i], side_slot + i, "side")
+        kept[i] = kept[i] + side_in[i].astype(jnp.float32)
+    hidden = jnp.concatenate(kept, axis=1) + rows_all[half, quarter, :].astype(jnp.float32)
     merged = rms_scale(hidden, merge_gain_ref[...].reshape(1, -1)).astype(jnp.bfloat16)
     merged_out[...] = merged.reshape(planes, share, depth)
 
@@ -923,7 +928,7 @@
     own_rows = asks_shape[1]
     group_rows = frame_rows // head_count
     share = group_rows // 4
-    messages = 9 + 11 * (seq_count // 2)
+    messages = 11 + 11 * (seq_count // 2)
     arguments = (
         patches,
         norm_gain,
@@ -960,10 +965,10 @@
             pltpu.VMEM((seq_count,) + asks_shape, bf16),
             pltpu.VMEM((frame_rows, 256), bf16),
             pltpu.VMEM((frame_rows, 256), bf16),
-            pltpu.VMEM((2 * group_rows, depth), bf16),
-            pltpu.VMEM((2 * group_rows, depth), bf16),
-            pltpu.VMEM((group_rows, depth), bf16),
-            pltpu.VMEM((group_rows, depth), bf16),
+            pltpu.VMEM((2, 2 * group_rows, depth // 2), bf16),
+            pltpu.VMEM((2, 2 * group_rows, depth // 2), bf16),
+            pltpu.VMEM((2, group_rows, depth // 2), bf16),
+            pltpu.VMEM((2, group_rows, depth // 2), bf16),
             pltpu.VMEM((planes, share, depth), bf16),
             pltpu.VMEM((planes, head_count, share, depth), bf16),
             pltpu.VMEM((planes, frame_rows // 4, kv_columns), jnp.float32),

time: 71.3 us -> 70.1 us (0.983)
  Pallas kernels: 70.5 us -> 69.3 us
    pallas_call x1, Pallas kernels: 70.5 us -> 69.3 us  [fused(): pl.pallas_call(functools.partial(fused_kernel, seq_count, head_count), ou...]
where the time goes in v4:
time: 70.1 us; the launch traced here: 69.9 us
  Pallas kernels  69.3 us (99%)
    pallas_call x1, Pallas kernels, fused(): pl.pallas_call(functools.partial(fused_kernel, seq_count, head_count), ou...  69.3 us

profile of v4, /device:TPU:0, one launch (start us, length us, event | category | flops | bytes accessed | tf_op | source)
XLA Modules:
  0.0 69.9 jit_solution(16589130226203456609)
XLA Ops:
  0.0 69.3 %fused.1 = bf16[2,2048]{1,0:T(2,128)(2,1)S(1)} custom-call(bf16[256,1280]{1,0:T(8,128)(2,1)} %patches_in.1, f32[1280]{0:T(1024)} %norm_gain_in.1, f32[1280]{0:T(1024)} %merge_gain_in.1, bf16[3,160,320]{2,1,0:T(8,128)(2,1)} %bitcast.3, bf16[160,320]{1,0:T(8,128)(2,1)} %bitcast.4, s32[1,64]{1,0:T(1,128)} %order_in.1, bf16[640,2,256]{2,1,0:T(2,128)(2,1)} %wkv_in.1, ...), custom_call_target="tpu_custom_call" | custom-call | tf_op jit(solution)/shard_map/fused/pallas_call | solution.py:945
  69.3 0.6 copy.13

commit v5 on v4

--- a/solution.py
+++ b/solution.py
@@ -698,8 +698,11 @@
         wo_hear(j)
     ask_slot, mix_slot, level_slot = (slots() for _ in range(3))
 
+    owners = [2 * target(k) + side for k in range(far) for side in (1 - y, y)]
+    owners.append(2 * z + 1 - y)
+
     def owner(step):
-        to = lax.rem(me + step, seq_count)
+        to = owners[step - 1]
         return to, {"seq": to, "head": head}
 
     send_all(seq_count, ask_slot, lambda step: (asks_ref, asks_all.at[me], owner(step)[1]))
@@ -844,12 +847,10 @@
         )
     mixed_in[me] = mixed_out[me]
     level_in[me] = level_out[...]
-    send_all(
-        seq_count,
-        mix_slot,
-        lambda step: (mixed_out.at[owner(step)[0]], mixed_in.at[me], owner(step)[1]),
-    )
-    send_all(seq_count, level_slot, lambda step: (level_out, level_in.at[me], owner(step)[1]))
+    for step in range(1, seq_count):
+        to, device = owner(step)
+        copy_of(level_out, level_in.at[me], device, level_slot, level_slot).start()
+        copy_of(mixed_out.at[to], mixed_in.at[me], device, mix_slot, mix_slot).start()
     arrived(mixed_in.at[others], mix_slot, "mix")
     arrived(level_in.at[others], level_slot, "level")
     row = lax.broadcasted_iota(jnp.int32, (own_rows, all_rows), 0)

time: 70.1 us -> 69.7 us (level)
  no operation moved by 1% of the time
where the time goes in v5:
time: 69.7 us; the launch traced here: 69.6 us
  Pallas kernels  69 us (99%)
    pallas_call x1, Pallas kernels, fused(): pl.pallas_call(functools.partial(fused_kernel, seq_count, head_count), ou...  69 us

profile of v5, /device:TPU:0, one launch (start us, length us, event | category | flops | bytes accessed | tf_op | source)
XLA Modules:
  0.0 69.6 jit_solution(13550310378061605467)
XLA Ops:
  0.0 69.0 %fused.1 = bf16[2,2048]{1,0:T(2,128)(2,1)S(1)} custom-call(bf16[256,1280]{1,0:T(8,128)(2,1)} %patches_in.1, f32[1280]{0:T(1024)} %norm_gain_in.1, f32[1280]{0:T(1024)} %merge_gain_in.1, bf16[3,160,320]{2,1,0:T(8,128)(2,1)} %bitcast.3, bf16[160,320]{1,0:T(8,128)(2,1)} %bitcast.4, s32[1,64]{1,0:T(1,128)} %order_in.1, bf16[640,2,256]{2,1,0:T(2,128)(2,1)} %wkv_in.1, ...), custom_call_target="tpu_custom_call" | custom-call | tf_op jit(solution)/shard_map/fused/pallas_call | solution.py:946
  69.0 0.6 copy.13
